TPU v7x, 256 devices: a whole 4x4x8 slice. The times are simulated.
256 devices in a mesh: dp: 8 (over z), expert: 4 (over y), tensor: 8 (over x, core).
Axes of the slice: x: 4, y: 4, z: 8, core: 2. Of those that a mesh axis runs over, the one named last changes fastest.
Arguments:
- tokens: bfloat16 [1024, 6144], P('dp', 'tensor'), may hold values from -6 to 6
- out_grad: bfloat16 [1024, 6144], P('dp', 'tensor'), may hold values from -6 to 6
- router_weight: bfloat16 [6144, 4], P('tensor'), may hold values from -0.078125 to 0.078125
- gate_weight: bfloat16 [4, 6144, 8192], P('expert', 'tensor', 'dp'), may hold values from -0.078125 to 0.078125
- up_weight: bfloat16 [4, 6144, 8192], P('expert', 'tensor', 'dp'), may hold values from -0.078125 to 0.078125
- down_weight: bfloat16 [4, 8192, 6144], P('expert', 'dp', 'tensor'), may hold values from -0.0625 to 0.0625
- expert_index: int32 [1024, 2], P('dp'), may hold values from 0 to 3, as said below
- slot_index: int32 [1024, 2], P('dp'), may hold values from 0 to 95, as said below
Outputs:
- tokens_grad: bfloat16 [1024, 6144], P(('dp', 'expert'), 'tensor')
- router_grad: float32 [6144, 4], P('tensor')
- gate_grad: bfloat16 [4, 6144, 8192], P('expert', 'tensor', 'dp')
- up_grad: bfloat16 [4, 6144, 8192], P('expert', 'tensor', 'dp')
- down_grad: bfloat16 [4, 8192, 6144], P('expert', 'dp', 'tensor')
Inputs may be any that keep to these rules, and one draw needn't show every extreme that they name: `expert_index`: each row names two different experts; in each aligned block of 128 rows no expert is named more than 96 times, and one expert is named exactly 96 times in every block. `slot_index`: entry k of a row is a slot of the expert in entry k of the same row of expert_index; within one aligned block of 128 rows the choices of one expert have distinct slots.
All inputs are finite; a program needn't handle non-finite values.
Results may differ from a plain program's by a relative error of at most 0.025.
Values may be sent and summed in bfloat16 or wider, within the bound.
A program may use at most 64 MiB of HBM per device.

v0:
```python
import math

import jax
import jax.numpy as jnp
from jax import lax
from jax.sharding import PartitionSpec as P

CAP = 96


def from_everyone(array, axis):
    count = lax.axis_size(axis)
    return lax.all_to_all(
        jnp.broadcast_to(array[None], (count, *array.shape)), axis, 0, 0, tiled=True
    )


def of_everyone(array, axis):
    return from_everyone(array, axis).sum(axis=0)


def sent_together(arrays, axis, dim, along):
    columns = [a.reshape(*a.shape[:along], -1) for a in arrays]
    both = jnp.concatenate(columns, axis=along)
    filled, at, gathered = (lax.all_gather(both, axis, axis=dim, tiled=True), 0, [])
    for a, column in zip(arrays, columns):
        slab = filled[..., at : at + column.shape[along]]
        gathered.append(slab.reshape(*slab.shape[:along], *a.shape[along:]))
        at += column.shape[along]
    return tuple(gathered)


def side_by_side(arrays, axis, dim, along):
    ends, at = ([], 0)
    for a in arrays[:-1]:
        at += a.shape[along]
        ends.append(at)
    both = jnp.concatenate(arrays, axis=along)
    return tuple(
        jnp.split(lax.psum_scatter(both, axis, scatter_dimension=dim, tiled=True), ends, axis=along)
    )


def side_by_side_2(arrays, axis, dim, along):
    both = jnp.concatenate(arrays, axis=along)
    filled, at, gathered = (lax.all_gather(both, axis, axis=dim, tiled=True), 0, [])
    for a in arrays:
        gathered.append(lax.slice_in_dim(filled, at, at + a.shape[along], axis=along))
        at += a.shape[along]
    return tuple(gathered)


def split_up(array, dim, count):
    before, after = (array.shape[:dim], array.shape[dim + 1 :])
    return jnp.moveaxis(array.reshape(*before, count, -1, *after), dim, 0)


def sent_and_summed(array, axis, dim):
    parts = split_up(array, dim, lax.axis_size(axis))
    arrived = lax.all_to_all(parts, axis, split_axis=0, concat_axis=0, tiled=True)
    return arrived.astype(jnp.float32).sum(axis=0)


def in_one_piece(arrays, axis, dim, along):
    widths = [math.prod(a.shape[along:]) for a in arrays]
    both = jnp.concatenate(
        [a.reshape(*a.shape[:along], w) for a, w in zip(arrays, widths)], axis=along
    )
    filled = sent_and_summed(both, axis, dim)
    parts = jnp.split(filled, [sum(widths[:k]) for k in range(1, len(widths))], axis=along)
    return tuple(
        (b.reshape(*filled.shape[:along], *a.shape[along:]) for a, b in zip(arrays, parts))
    )


def in_one_piece_2(arrays, axis, dim, along):
    both = jnp.concatenate(arrays, axis=along)
    filled, at, gathered = (sent_and_summed(both, axis, dim), 0, [])
    for a in arrays:
        gathered.append(lax.slice_in_dim(filled, at, at + a.shape[along], axis=along))
        at += a.shape[along]
    return tuple(gathered)


def contract_rows(left_side, right_side):
    return lax.dot_general(
        left_side, right_side, (((0,), (0,)), ((), ())), preferred_element_type=jnp.float32
    )


def contract_cols(left_side, right_side):
    return lax.dot_general(
        left_side, right_side, (((1,), (1,)), ((), ())), preferred_element_type=jnp.float32
    )


def split_parts(values):
    high_part = values.astype(jnp.bfloat16)
    low_part = (values - high_part.astype(jnp.float32)).astype(jnp.bfloat16)
    return (high_part, low_part)


def table_apply(form, table_low, values):
    high_part, low_part = split_parts(values)
    return jnp.einsum(form, table_low, high_part, preferred_element_type=jnp.float32) + jnp.einsum(
        form, table_low, low_part, preferred_element_type=jnp.float32
    )


def slot_table(experts_here, slots_here, expert_id, capacity):
    positions = lax.broadcasted_iota(jnp.int32, (capacity, experts_here.shape[0]), 0)
    first_table = (experts_here[:, 0] == expert_id)[None, :] & (
        slots_here[:, 0][None, :] == positions
    )
    second_table = (experts_here[:, 1] == expert_id)[None, :] & (
        slots_here[:, 1][None, :] == positions
    )
    return (first_table.astype(jnp.float32), second_table.astype(jnp.float32))


def hidden_terms(gate_sum, up_sum, grad_act, slot_prob):
    gate_sigmoid = jax.nn.sigmoid(gate_sum)
    hidden = (gate_sum * gate_sigmoid * up_sum).astype(jnp.bfloat16)
    prob_grad = jnp.sum(hidden.astype(jnp.float32) * grad_act, axis=1)
    act_grad = slot_prob.astype(jnp.float32)[:, None] * grad_act
    grad_gate = (act_grad * up_sum * gate_sigmoid * (1.0 + gate_sum * (1.0 - gate_sigmoid))).astype(
        jnp.bfloat16
    )
    grad_up = (act_grad * gate_sum * gate_sigmoid).astype(jnp.bfloat16)
    return (hidden, grad_gate, grad_up, prob_grad)


def shards(
    tokens, out_grad, router_weight, gate_weight, up_weight, down_weight, expert_index, slot_index
):
    capacity = CAP
    expert_count = router_weight.shape[1]
    expert_id = lax.axis_index("expert")
    logits = of_everyone(
        jnp.dot(tokens, router_weight, preferred_element_type=jnp.float32), "tensor"
    )
    chosen = jnp.take_along_axis(logits, expert_index, axis=1)
    pick_prob = jnp.stack(
        [jax.nn.sigmoid(chosen[:, 0] - chosen[:, 1]), jax.nn.sigmoid(chosen[:, 1] - chosen[:, 0])],
        axis=1,
    )
    prob_wide = pick_prob.astype(jnp.bfloat16).astype(jnp.float32)
    first_table, second_table = slot_table(expert_index, slot_index, expert_id, capacity)
    select = first_table + second_table
    select_low = select.astype(jnp.bfloat16)
    local_tokens = jnp.dot(select_low, tokens, preferred_element_type=jnp.float32).astype(
        jnp.bfloat16
    )
    local_grads = jnp.dot(select_low, out_grad, preferred_element_type=jnp.float32).astype(
        jnp.bfloat16
    )
    local_prob = (
        jnp.dot(first_table, prob_wide[:, 0]) + jnp.dot(second_table, prob_wide[:, 1])
    ).astype(jnp.bfloat16)
    slot_tokens, slot_grads, slot_prob = sent_together(
        (local_tokens, local_grads, local_prob), "dp", 0, 1
    )
    gate_block = gate_weight[0]
    up_block = up_weight[0]
    down_block = down_weight[0]
    gate_part = jnp.dot(slot_tokens, gate_block, preferred_element_type=jnp.float32)
    up_part = jnp.dot(slot_tokens, up_block, preferred_element_type=jnp.float32)
    grad_part = contract_cols(slot_grads, down_block)
    slot_count = slot_tokens.shape[0]
    share_rows = slot_count // lax.axis_size("tensor")
    share_start = lax.axis_index("tensor") * share_rows
    gate_share, up_share, grad_share = tuple(
        (
            part.astype(jnp.float32)
            for part in side_by_side(
                (
                    gate_part.astype(jnp.bfloat16),
                    up_part.astype(jnp.bfloat16),
                    grad_part.astype(jnp.bfloat16),
                ),
                "tensor",
                0,
                1,
            )
        )
    )
    prob_share = lax.dynamic_slice_in_dim(slot_prob, share_start, share_rows, 0)
    hidden_share, gate_share_grad, up_share_grad, prob_grad_share = hidden_terms(
        gate_share, up_share, grad_share, prob_share
    )
    hidden, grad_gate, grad_up = side_by_side_2(
        (hidden_share, gate_share_grad, up_share_grad), "tensor", 0, 1
    )
    prob_grad = lax.dynamic_update_slice_in_dim(
        jnp.zeros((slot_count,), jnp.float32), prob_grad_share, share_start, 0
    )
    scaled_grads = (slot_prob.astype(jnp.float32)[:, None] * slot_grads.astype(jnp.float32)).astype(
        jnp.bfloat16
    )
    down_grad = contract_rows(hidden, scaled_grads).astype(jnp.bfloat16)
    gate_grad = contract_rows(slot_tokens, grad_gate).astype(jnp.bfloat16)
    up_grad = contract_rows(slot_tokens, grad_up).astype(jnp.bfloat16)
    slot_dx = contract_cols(grad_gate, gate_block) + contract_cols(grad_up, up_block)
    own_expert = (lax.broadcasted_iota(jnp.int32, (1, expert_count), 1) == expert_id).astype(
        jnp.float32
    )
    row_dx, row_prob = in_one_piece(
        (slot_dx.astype(jnp.bfloat16), prob_grad.astype(jnp.bfloat16)), "dp", 0, 1
    )
    token_dx = table_apply("cn,cd->nd", select_low, row_dx)
    token_prob = table_apply("cn,c->n", select_low, row_prob)
    token_term, prob_rows = in_one_piece_2(
        (token_dx.astype(jnp.bfloat16), (token_prob[:, None] * own_expert).astype(jnp.bfloat16)),
        "expert",
        0,
        1,
    )
    prob_rows = of_everyone(prob_rows, "tensor")
    quarter = token_term.shape[0]
    offset = expert_id * quarter
    part_prob = lax.dynamic_slice_in_dim(pick_prob, offset, quarter, 0)
    part_experts = lax.dynamic_slice_in_dim(expert_index, offset, quarter, 0)
    part_tokens = lax.dynamic_slice_in_dim(tokens, offset, quarter, 0)
    pick_grad = jnp.take_along_axis(prob_rows, part_experts, axis=1)
    mixed_grad = jnp.sum(part_prob * pick_grad, axis=1, keepdims=True)
    weights = part_prob * (pick_grad - mixed_grad)
    onehot = (
        part_experts[:, :, None] == lax.broadcasted_iota(jnp.int32, (1, 1, expert_count), 2)
    ).astype(jnp.float32)
    logit_grad = jnp.sum(onehot * weights[:, :, None], axis=1)
    router_rows = router_weight.astype(jnp.float32)
    tokens_grad = (token_term + jnp.dot(logit_grad, router_rows.T)).astype(jnp.bfloat16)
    router_part = jnp.dot(part_tokens.astype(jnp.float32).T, logit_grad)
    router_grad = of_everyone(router_part, ("dp", "expert"))
    return (tokens_grad, router_grad, gate_grad[None], up_grad[None], down_grad[None])


def solution(mesh):
    in_specs = (
        P("dp", "tensor"),
        P("dp", "tensor"),
        P("tensor", None),
        P("expert", "tensor", "dp"),
        P("expert", "tensor", "dp"),
        P("expert", "dp", "tensor"),
        P("dp", None),
        P("dp", None),
    )
    out_specs = (
        P(("dp", "expert"), "tensor"),
        P("tensor", None),
        P("expert", "tensor", "dp"),
        P("expert", "tensor", "dp"),
        P("expert", "dp", "tensor"),
    )
    return jax.shard_map(shards, mesh=mesh, in_specs=in_specs, out_specs=out_specs, check_vma=False)
```

profile of v0, /device:TPU:1, one launch (start us, length us, event | category | flops | bytes accessed | tf_op | source)
XLA Modules:
  0.0 257.2 jit_solution(16779585894869591958)
XLA Ops:
  7.2 1.2 fusion.66
  8.3 0.7 broadcast_in_dim.22
  9.0 6.4 %all-to-all-start = ((f32[8,128,4]{1,2,0:T(4,128)}), f32[8,128,4]{1,2,0:T(4,128)S(1)}, u32[]{:S(2)}, u32[]{:S(2)}) async-start(f32[8,128,4]{1,2,0:T(4,128)} %broadcast_in_dim.22), calls=%async_computation | async-start | bytes 32768 | tf_op jit(solution)/shard_map/all_to_all | solution.py:13
  15.5 0.8 slice_bitcast_fusion.1
  16.2 0.8 compare_bitcast_fusion.1
  17.0 1.1 convolution_convert_fusion.7
  18.1 1.1 convolution_convert_fusion.6
  19.2 0.7 bitcast_or_fusion.1
  20.2 2.4 gather_fusion
  23.3 0.8 pad_maximum_fusion.3
  24.1 40.8 %all-gather.3.cloned.1.call-done = bf16[768,1537]{1,0:T(8,128)(2,1)} async-done(((bf16[96,1537]{1,0:T(8,128)(2,1)}), bf16[768,1537]{1,0:T(8,128)(2,1)}) %all-gather.3.cloned.1.call-update) | async-done | bytes 2360848 | tf_op jit(solution)/shard_map/all_gather | solution.py:25
  64.9 3.3 %convolution_convert_fusion.3 = bf16[768,1024]{1,0:T(8,128)(2,1)S(1)} fusion(bf16[1,1024,768]{2,1,0:T(8,128)(2,1)} %param.13, bf16[768,1537]{1,0:T(8,128)(2,1)} %all-gather.3.cloned.1.call-done), kind=kOutput, calls=%fused_computation.9 | convolution fusion | flops 1208745984 | bytes 4325376 | tf_op jit(solution)/shard_map/dot_general | solution.py:92
  68.2 1.4 convolution_convert_fusion.4
  69.7 1.4 convolution_convert_fusion.5
  71.1 2.3 pad_maximum_fusion
  73.4 0.8 slice-done
  74.4 39.9 %reduce-scatter.2.cloned.1.call-done = bf16[96,3072]{1,0:T(8,128)(2,1)} async-done(((bf16[768,3072]{1,0:T(8,128)(2,1)}), bf16[96,3072]{1,0:T(8,128)(2,1)}) %reduce-scatter.2.cloned.1.call-update) | async-done | bytes 589840 | tf_op jit(solution)/shard_map/reduce_scatter | solution.py:40
  114.3 1.6 fusion.35
  115.9 0.9 pad_maximum_fusion.2
  116.8 0.2 dynamic_update_slice.3
  117.0 0.3 concatenate.33
  117.3 38.6 %all-gather.5.cloned.1.call-done = bf16[768,3072]{1,0:T(8,128)(2,1)} async-done(((bf16[96,3072]{1,0:T(8,128)(2,1)}), bf16[768,3072]{1,0:T(8,128)(2,1)}) %all-gather.5.cloned.1.call-update) | async-done | bytes 4718608 | tf_op jit(solution)/shard_map/all_gather | solution.py:46
  156.0 2.9 %fusion.2 = f32[768,768]{1,0:T(8,128)S(1)} fusion(bf16[1,768,1024]{2,1,0:T(8,128)(2,1)S(1)} %copy-done, bf16[768,3072]{1,0:T(8,128)(2,1)} %all-gather.5.cloned.1.call-done), kind=kOutput, calls=%fused_computation.14 | convolution fusion | flops 1207959552 | bytes 5505024 | tf_op jit(solution)/shard_map/dot_general | solution.py:92
  158.9 2.9 %add_convert_fusion = bf16[768,768]{1,0:T(8,128)(2,1)S(1)} fusion(f32[768,768]{1,0:T(8,128)S(1)} %fusion.2, bf16[1,768,1024]{2,1,0:T(8,128)(2,1)S(1)} %copy-done.6, bf16[768,3072]{1,0:T(8,128)(2,1)} %all-gather.5.cloned.1.call-done), kind=kOutput, calls=%fused_computation.5 | convolution fusion | flops 1209139200 | bytes 6684672 | tf_op jit(solution)/shard_map/dot_general | solution.py:92
  161.8 1.2 pad_maximum_fusion.1
  163.0 6.7 %all-to-all-start.1 = ((bf16[8,96,769]{2,1,0:T(8,128)(2,1)}), bf16[8,96,769]{2,1,0:T(8,128)(2,1)S(1)}, u32[]{:S(2)}, u32[]{:S(2)}) async-start(bf16[8,96,769]{2,1,0:T(8,128)(2,1)} %pad_maximum_fusion.1), calls=%async_computation.2 | async-start | bytes 2752512 | tf_op jit(solution)/shard_map/all_to_all | solution.py:60
  170.0 36.0 %all-to-all-done.1 = bf16[8,96,769]{2,1,0:T(8,128)(2,1)S(1)} async-done(((bf16[8,96,769]{2,1,0:T(8,128)(2,1)}), bf16[8,96,769]{2,1,0:T(8,128)(2,1)S(1)}, u32[]{:S(2)}, u32[]{:S(2)}) %all-to-all-start.1) | async-done | bytes 1181216 | tf_op jit(solution)/shard_map/all_to_all | solution.py:60
  206.2 0.2 fusion.43
  206.6 0.3 fusion.20
  207.3 0.7 pad_maximum_fusion.4
  208.0 4.0 %all-to-all-start.2 = ((bf16[4,32,772]{2,1,0:T(8,128)(2,1)}), bf16[4,32,772]{2,1,0:T(8,128)(2,1)S(1)}, u32[]{:S(2)}, u32[]{:S(2)}) async-start(bf16[4,32,772]{2,1,0:T(8,128)(2,1)} %bitcast.18), calls=%async_computation.3 | async-start | bytes 458752 | tf_op jit(solution)/shard_map/all_to_all | solution.py:60
  212.1 1.1 convert_reduce_fusion.2
  213.1 4.3 %all-to-all-done.2 = bf16[4,32,772]{2,1,0:T(8,128)(2,1)S(1)} async-done(((bf16[4,32,772]{2,1,0:T(8,128)(2,1)}), bf16[4,32,772]{2,1,0:T(8,128)(2,1)S(1)}, u32[]{:S(2)}, u32[]{:S(2)}) %all-to-all-start.2) | async-done | bytes 197664 | tf_op jit(solution)/shard_map/all_to_all | solution.py:60
  217.6 0.7 reshape.114
  218.2 5.1 %all-to-all-start.3 = ((f32[8,1,128]{2,1,0:T(1,128)}), f32[8,1,128]{2,1,0:T(1,128)S(1)}, u32[]{:S(2)}, u32[]{:S(2)}) async-start(f32[8,1,128]{2,1,0:T(1,128)} %reshape.114), calls=%async_computation.4 | async-start | bytes 8192 | tf_op jit(solution)/shard_map/all_to_all | solution.py:13
  223.4 4.3 %fusion.8 = bf16[1,768,1024]{2,1,0:T(8,128)(2,1)} fusion(bf16[768,3072]{1,0:T(8,128)(2,1)} %all-gather.5.cloned.1.call-done, bf16[768,1537]{1,0:T(8,128)(2,1)} %all-gather.3.cloned.1.call-done), kind=kOutput, calls=%fused_computation.20 | convolution fusion | flops 1208745984 | bytes 4325376 | tf_op jit(solution)/shard_map/dot_general | solution.py:86
  227.7 0.2 all-to-all-done.3
  227.9 0.5 broadcast.97
  228.4 0.7 reduce.6
  229.2 0.9 gather_fusion.1
  230.4 0.9 fusion.44
  231.4 0.8 broadcast_in_dim.27
  232.2 4.1 %all-to-all-start.4 = ((f32[32,768,4]{1,2,0:T(4,128)}), f32[32,768,4]{1,2,0:T(4,128)S(1)}, u32[]{:S(2)}, u32[]{:S(2)}) async-start(f32[32,768,4]{1,2,0:T(4,128)} %broadcast_in_dim.27), calls=%async_computation.5 | async-start | bytes 786432 | tf_op jit(solution)/shard_map/all_to_all | solution.py:13
  236.2 4.5 %fusion.9 = bf16[1,768,1024]{2,1,0:T(8,128)(2,1)} fusion(bf16[768,3072]{1,0:T(8,128)(2,1)} %all-gather.5.cloned.1.call-done, bf16[768,1537]{1,0:T(8,128)(2,1)} %all-gather.3.cloned.1.call-done), kind=kOutput, calls=%fused_computation.21 | convolution fusion | flops 1208745984 | bytes 4325376 | tf_op jit(solution)/shard_map/dot_general | solution.py:86
  240.7 4.1 %fusion.10 = bf16[1,1024,768]{2,1,0:T(8,128)(2,1)} fusion(bf16[768,3072]{1,0:T(8,128)(2,1)} %all-gather.5.cloned.1.call-done, f32[768]{0:T(1024)S(1)} %convert_reduce_fusion.2, bf16[768,1537]{1,0:T(8,128)(2,1)S(1)} %copy-done.2), kind=kOutput, calls=%fused_computation.22 | convolution fusion | flops 1210515456 | bytes 4329472 | tf_op jit(solution)/shard_map/dot_general | solution.py:86
  244.8 0.8 fusion.21
  245.7 4.3 %all-to-all-done.4 = f32[32,768,4]{1,2,0:T(4,128)S(1)} async-done(((f32[32,768,4]{1,2,0:T(4,128)}), f32[32,768,4]{1,2,0:T(4,128)S(1)}, u32[]{:S(2)}, u32[]{:S(2)}) %all-to-all-start.4) | async-done | bytes 393248 | tf_op jit(solution)/shard_map/all_to_all | solution.py:13
  250.0 0.7 reduce_sum.79
  (57 shorter events, 2.9 us)
Async XLA Ops:
  7.2 61.0 %copy-start = (bf16[1,768,1024]{2,1,0:T(8,128)(2,1)S(1)}, bf16[1,768,1024]{2,1,0:T(8,128)(2,1)}, u32[]{:S(2)}) copy-start(bf16[1,768,1024]{2,1,0:T(8,128)(2,1)} %param.12) | copy-start | bytes 4718596
  9.0 11.1 %all-to-all-start = ((f32[8,128,4]{1,2,0:T(4,128)}), f32[8,128,4]{1,2,0:T(4,128)S(1)}, u32[]{:S(2)}, u32[]{:S(2)}) async-start(f32[8,128,4]{1,2,0:T(4,128)} %broadcast_in_dim.22), calls=%async_computation | async-start | bytes 32768 | tf_op jit(solution)/shard_map/all_to_all | solution.py:13
  15.5 49.4 %all-gather.3.cloned.1.call-start = ((), (), s32[]{:S(2)}) async-start(), calls=%async_computation.6 | async-start | bytes 2875392 | tf_op jit(solution)/shard_map/all_gather | solution.py:25
  20.2 2.6 %copy-start.4 = (s32[128,2]{0,1:T(2,128)S(1)}, s32[128,2]{0,1:T(2,128)}, u32[]{:S(2)}) copy-start(s32[128,2]{0,1:T(2,128)} %param.14) | copy-start | bytes 3076
  24.0 90.3 %reduce-scatter.2.cloned.1.call-start = ((), (), s32[]{:S(2)}) async-start(), calls=%async_computation.7 | async-start | bytes 5308416 | tf_op jit(solution)/shard_map/reduce_scatter | solution.py:40
  64.9 3.4 %copy-start.1 = (bf16[768,1537]{1,0:T(8,128)(2,1)S(1)}, bf16[768,1537]{1,0:T(8,128)(2,1)}, u32[]{:S(2)}) copy-start(bf16[768,1537]{1,0:T(8,128)(2,1)} %all-gather.3.cloned.1.call-done) | copy-start | bytes 7082500
  68.2 1.4 copy-start.5
  73.4 0.9 slice-start
  73.4 82.6 %all-gather.5.cloned.1.call-start = ((), (), s32[]{:S(2)}) async-start(), calls=%async_computation.8 | async-start | bytes 5308416 | tf_op jit(solution)/shard_map/all_gather | solution.py:46
  156.0 3.0 %copy-start.6 = (bf16[1,768,1024]{2,1,0:T(8,128)(2,1)S(1)}, bf16[1,768,1024]{2,1,0:T(8,128)(2,1)}, u32[]{:S(2)}) copy-start(bf16[1,768,1024]{2,1,0:T(8,128)(2,1)} %param.11) | copy-start | bytes 4718596
  163.0 43.0 %all-to-all-start.1 = ((bf16[8,96,769]{2,1,0:T(8,128)(2,1)}), bf16[8,96,769]{2,1,0:T(8,128)(2,1)S(1)}, u32[]{:S(2)}, u32[]{:S(2)}) async-start(bf16[8,96,769]{2,1,0:T(8,128)(2,1)} %pad_maximum_fusion.1), calls=%async_computation.2 | async-start | bytes 2752512 | tf_op jit(solution)/shard_map/all_to_all | solution.py:60
  208.0 9.4 %all-to-all-start.2 = ((bf16[4,32,772]{2,1,0:T(8,128)(2,1)}), bf16[4,32,772]{2,1,0:T(8,128)(2,1)S(1)}, u32[]{:S(2)}, u32[]{:S(2)}) async-start(bf16[4,32,772]{2,1,0:T(8,128)(2,1)} %bitcast.18), calls=%async_computation.3 | async-start | bytes 458752 | tf_op jit(solution)/shard_map/all_to_all | solution.py:60
  218.2 9.6 %all-to-all-start.3 = ((f32[8,1,128]{2,1,0:T(1,128)}), f32[8,1,128]{2,1,0:T(1,128)S(1)}, u32[]{:S(2)}, u32[]{:S(2)}) async-start(f32[8,1,128]{2,1,0:T(1,128)} %reshape.114), calls=%async_computation.4 | async-start | bytes 8192 | tf_op jit(solution)/shard_map/all_to_all | solution.py:13
  232.2 17.8 %all-to-all-start.4 = ((f32[32,768,4]{1,2,0:T(4,128)}), f32[32,768,4]{1,2,0:T(4,128)S(1)}, u32[]{:S(2)}, u32[]{:S(2)}) async-start(f32[32,768,4]{1,2,0:T(4,128)} %broadcast_in_dim.27), calls=%async_computation.5 | async-start | bytes 786432 | tf_op jit(solution)/shard_map/all_to_all | solution.py:13
  236.2 4.5 %copy-start.2 = (bf16[768,1537]{1,0:T(8,128)(2,1)S(1)}, bf16[768,1537]{1,0:T(8,128)(2,1)}, u32[]{:S(2)}) copy-start(bf16[768,1537]{1,0:T(8,128)(2,1)} %all-gather.3.cloned.1.call-done) | copy-start | bytes 7082500
  240.7 4.1 %copy-start.3 = (bf16[768,4]{0,1:T(4,128)(2,1)S(1)}, bf16[768,4]{0,1:T(4,128)(2,1)}, u32[]{:S(2)}) copy-start(bf16[768,4]{0,1:T(4,128)(2,1)} %param.10) | copy-start | bytes 18436
Sparse Core Ops, SparseCore 0:
  24.2 40.6 all-gather.2
  73.5 40.7 reduce-scatter.1
  116.9 39.0 all-gather.4
where the time goes:
time: 259 us; the launch traced here: 257 us
  waiting for transfers between devices  164 us (63%)
  matrix products  31.1 us (12%)
  starting transfers between devices  26.4 us (10%)
  between operations  14 us (5%)
  other arithmetic  12 us (5%)
  local copies, waits for them, and re-layouts  9.51 us (4%)
    all_gather x1, waiting for transfers between devices, sent_together(): lax.all_gather(both, axis, axis=dim, tiled=True)  40.8 us
    all_to_all x2, waiting for transfers between devices, sent_and_summed(): lax.all_to_all(parts, axis, split_axis=0, concat_axis=0, tiled=True)  40.3 us
    reduce_scatter x1, waiting for transfers between devices, side_by_side(): lax.psum_scatter(both, axis, scatter_dimension=dim, tiled=True)  39.9 us
    all_gather x1, waiting for transfers between devices, side_by_side_2(): lax.all_gather(both, axis, axis=dim, tiled=True)  38.6 us
    all_to_all x3, starting transfers between devices, from_everyone(): lax.all_to_all(jnp.broadcast_to(array[None], (count, *array.shape)), axis...  15.6 us
    dot_general x3, matrix products, contract_rows(): lax.dot_general(left_side, right_side, (((0,), (0,)), ((), ())), preferre...  12.9 us
    all_to_all x2, starting transfers between devices, sent_and_summed(): lax.all_to_all(parts, axis, split_axis=0, concat_axis=0, tiled=True)  10.7 us
    dot_general x3, matrix products, contract_cols(): lax.dot_general(left_side, right_side, (((1,), (1,)), ((), ())), preferre...  9.16 us
  transfers between devices with their start and end apart: 8, of which 7 were waited for; matrix products, arithmetic and copies ran while one was open for 8% of the time, Pallas kernels for 0%

commit v1 on v0

v1 whole, which is shorter than its diff:
```python
import jax
import jax.numpy as jnp
from jax import lax
from jax.experimental import pallas as pl
from jax.experimental.pallas import tpu as pltpu
from jax.sharding import PartitionSpec as P

CAP = 96
MESH = pl.DeviceIdType.MESH
F32 = jnp.float32
BF16 = jnp.bfloat16

ORDER = (0, -1, 1, -2, 2, 4, -3, 3)
GROUPS = (1, 2, 2, 1, 2)
POS = {o: i for i, o in enumerate(ORDER)}


def place(offset):
    o = offset % 8
    return POS[o if o <= 4 else o - 8]


CHUNKS = []
_at = 0
for _n in GROUPS:
    CHUNKS.append((_at, _n))
    _at += _n

STAGES = ("F", "R1", "R2", "E", "G1", "G2", "X")
SKEW = 2


def plan():
    steps = []
    last = len(STAGES) + SKEW * (len(CHUNKS) - 1)
    for s in range(last):
        for k in range(len(CHUNKS)):
            i = s - SKEW * k
            if 0 <= i < len(STAGES):
                steps.append((STAGES[i], k))
    return steps


def dot_nt(a, b):
    return lax.dot_general(a, b, (((1,), (1,)), ((), ())), preferred_element_type=F32)


def dot_nn(a, b):
    return lax.dot_general(a, b, (((1,), (0,)), ((), ())), preferred_element_type=F32)


class Copies:
    def __init__(self, send, recv):
        self.send, self.recv, self.count, self.made = send, recv, 0, {}

    def add(self, name, src, dst, device):
        i = self.count
        self.count += 1
        c = pltpu.make_async_remote_copy(
            src_ref=src,
            dst_ref=dst,
            send_sem=self.send.at[i],
            recv_sem=self.recv.at[i],
            device_id=device,
            device_id_type=MESH,
        )
        self.made[name] = c
        c.start()

    def got(self, name):
        self.made[name].wait_recv()

    def drain(self):
        for c in self.made.values():
            c.wait_send()


N_COPIES = 160


def kernel(
    tok_in, og_in, rwt, idx, gw_h, uw_h, dw_h,
    gg_h, ug_h, dg_h, rowdx, rowprob, picks,
    tk, gr, sc, tkt, gw, uw, dw, part, dbuf, fa, fb, rl, rr, hh, h0t, pcol,
    lgs, lgr, prs, prr, dps, dpr, dxs, dxr, dxo, wout,
    send_sem, recv_sem, wsem, osem,
):
    z = lax.axis_index("dp")
    y = lax.axis_index("expert")
    t = lax.axis_index("tensor")
    x = t // 2
    c = t % 2
    right, left = (x + 1) % 4, (x + 3) % 4
    across = (x + 2) % 4
    t_right, t_left, t_sib = right * 2 + c, left * 2 + c, x * 2 + (1 - c)

    wcopies = [
        pltpu.make_async_copy(a, b, wsem.at[i])
        for i, (a, b) in enumerate(((gw_h, gw), (uw_h, uw), (dw_h, dw)))
    ]
    for w in wcopies:
        w.start()

    barrier = pltpu.get_barrier_semaphore()
    for k in range(1, 8):
        pl.semaphore_signal(barrier, inc=1, device_id={"dp": (z + k) % 8}, device_id_type=MESH)
        pl.semaphore_signal(barrier, inc=1, device_id={"tensor": (t + k) % 8}, device_id_type=MESH)
    pl.semaphore_wait(barrier, 14)

    cp = Copies(send_sem, recv_sem)

    slot_at = lax.broadcasted_iota(jnp.int32, (CAP, 128), 0)
    lane_at = lax.broadcasted_iota(jnp.int32, (CAP, 128), 1)
    eye = (slot_at == lane_at).astype(F32)
    e0, e1, s0, s1 = idx[0:1, :], idx[1:2, :], idx[2:3, :], idx[3:4, :]
    table0 = jnp.where((e0 == y) & (s0 == slot_at), 1.0, 0.0).astype(F32)
    table1 = jnp.where((e1 == y) & (s1 == slot_at), 1.0, 0.0).astype(F32)
    select = (table0 + table1).astype(BF16)

    tk[0:CAP, :] = dot_nn(select, tok_in[...]).astype(BF16)
    gr[0:CAP, :] = dot_nn(select, og_in[...]).astype(BF16)

    def rows_of(p):
        return pl.ds(p * CAP, CAP)

    def ring(step, which):
        buf = tk if which == "t" else gr
        cp.add(("r", step + 1, which), buf.at[rows_of(place(-step))],
               buf.at[rows_of(place(-step - 1))], {"dp": (z + 1) % 8})

    def ring_back(step, which):
        buf = tk if which == "t" else gr
        cp.add(("l", step + 1, which), buf.at[rows_of(place(step))],
               buf.at[rows_of(place(step + 1))], {"dp": (z + 7) % 8})

    for which in "tg":
        ring(0, which)
        ring_back(0, which)

    lgs[...] = dot_nt(rwt[...], tok_in[...])
    for k in range(1, 8):
        cp.add(("lg", k), lgs, lgr.at[k], {"tensor": (t + k) % 8})

    def probabilities():
        total = lgs[...]
        for k in range(1, 8):
            cp.got(("lg", k))
            total = total + lgr[k]
        l0 = jnp.zeros((1, 128), F32)
        l1 = jnp.zeros((1, 128), F32)
        for j in range(4):
            l0 = l0 + jnp.where(e0 == j, total[j : j + 1, :], 0.0)
            l1 = l1 + jnp.where(e1 == j, total[j : j + 1, :], 0.0)
        p0 = jax.nn.sigmoid(l0 - l1)
        p1 = jax.nn.sigmoid(l1 - l0)
        picks[0:1, :] = p0
        picks[1:2, :] = p1
        low0 = p0.astype(BF16).astype(F32)
        low1 = p1.astype(BF16).astype(F32)
        col = jnp.sum(table0 * low0 + table1 * low1, axis=1, keepdims=True)
        pcol[0:CAP, :] = col
        prs[...] = jnp.broadcast_to(jnp.sum(eye * col, axis=0, keepdims=True), (8, 128))
        for k in range(1, 8):
            cp.add(("pr", k), prs, prr.at[place(-k)], {"dp": (z + k) % 8})

    def probability_of(p):
        o = ORDER[p]
        if o == 0:
            return
        cp.got(("pr", (-o) % 8))
        col = jnp.sum(eye * prr[p][0:1, :], axis=1, keepdims=True)
        pcol[p * CAP : (p + 1) * CAP, :] = col

    def arrive(p):
        o = ORDER[p]
        if o == 0:
            return
        if o == 4:
            cp.got(("r", 4, "t"))
            cp.got(("l", 4, "g"))
            return
        d = abs(o)
        for which in "tg":
            cp.got(("r" if o < 0 else "l", d, which))
            if o < 0:
                if d < 3 or which == "t":
                    ring(d, which)
            else:
                if d < 3 or which == "g":
                    ring_back(d, which)

    arrived = set()

    def arrive_all(ps):
        for p in ps:
            if p not in arrived:
                arrived.add(p)
                arrive(p)

    first = [True]

    def stage_f(k):
        p0, n = CHUNKS[k]
        r0, r = p0 * CAP, n * CAP
        for p in range(p0, p0 + n):
            if ORDER[p] == 4:
                arrive_all([POS[-3], POS[3]])
            arrive_all([p])
        if first[0]:
            for w in wcopies:
                w.wait()
            first[0] = False
        rows = pl.ds(r0, r)
        a = tk[r0 : r0 + r, :]
        b = gr[r0 : r0 + r, :]

        @pl.loop(0, 4)
        def _(n):
            cols = pl.ds(pl.multiple_of(n * 256, 256), 256)
            for m, v in enumerate((
                dot_nn(a, gw[:, cols]), dot_nn(a, uw[:, cols]), dot_nt(b, dw[cols, :]),
            )):
                v = v.astype(BF16)
                part[0, n, rows, m * 128 : m * 128 + 128] = v[:, 0:128]
                part[1, n, rows, m * 128 : m * 128 + 128] = v[:, 128:256]

        cp.add(("d2d", k), part.at[1 - c, :, rows, :], dbuf.at[:, rows, :], {"tensor": t_sib})

    def halves(k):
        p0, n = CHUNKS[k]
        r0, r = p0 * CAP, n * CAP
        h = r // 2
        return slice(r0, r0 + h), slice(r0 + h, r0 + r), pl.ds(r0, h), pl.ds(r0 + h, h)

    def fold(target, rows):
        v = part[c, target, rows, :].astype(F32) + dbuf[target, rows, :].astype(F32)
        part[c, target, rows, :] = v.astype(BF16)

    def stage_r1(k):
        sa, sb, da, db = halves(k)
        cp.got(("d2d", k))
        fold(across, sa)
        cp.add(("fa", k), part.at[c, across, da, :], fa.at[da, :], {"tensor": t_right})
        fold(across, sb)
        cp.add(("fb", k), part.at[c, across, db, :], fb.at[db, :], {"tensor": t_left})
        fold(right, sb)
        cp.add(("rlb", k), part.at[c, right, db, :], rl.at[db, :], {"tensor": t_right})
        fold(left, sa)
        cp.add(("rra", k), part.at[c, left, da, :], rr.at[da, :], {"tensor": t_left})

    def fold2(target, rows, extra):
        v = part[c, target, rows, :].astype(F32) + dbuf[target, rows, :].astype(F32)
        v = v + extra[rows, :].astype(F32)
        part[c, target, rows, :] = v.astype(BF16)

    def stage_r2(k):
        sa, sb, da, db = halves(k)
        cp.got(("fa", k))
        fold2(right, sa, fa)
        cp.add(("rla", k), part.at[c, right, da, :], rl.at[da, :], {"tensor": t_right})
        cp.got(("fb", k))
        fold2(left, sb, fb)
        cp.add(("rrb", k), part.at[c, left, db, :], rr.at[db, :], {"tensor": t_left})

    def tcols(q):
        return pl.ds(pl.multiple_of(q * 128, 128), 128)

    def h_copy(name, rows, q, device):
        ref = hh.at[:, rows, tcols(q)]
        cp.add(name, ref, ref, {"tensor": device})

    def stage_e(k):
        p0, n = CHUNKS[k]
        sa, sb, da, db = halves(k)
        for p in range(p0, p0 + n):
            probability_of(p)
        for s, names in ((sb, ("rlb", "rrb")), (sa, ("rla", "rra"))):
            for q in names:
                cp.got((q, k))
            v = part[c, x, s, :].astype(F32) + dbuf[x, s, :].astype(F32)
            v = v + rl[s, :].astype(F32) + rr[s, :].astype(F32)
            gate, up, ga = v[:, 0:128], v[:, 128:256], v[:, 256:384]
            g = jax.nn.sigmoid(gate)
            hid = (gate * g * up).astype(BF16)
            pcol_s = pcol[s, :]
            a = pcol_s * ga
            hh[0, s, tcols(t)] = hid
            hh[1, s, tcols(t)] = (a * up * g * (1.0 + gate * (1.0 - g))).astype(BF16)
            hh[2, s, tcols(t)] = (a * gate * g).astype(BF16)
            dpc = jnp.sum(hid.astype(F32) * ga, axis=1, keepdims=True)
            dprob_parts[(k, s.start)] = dpc
        h_copy(("ra", k), da, t, t_right)
        h_copy(("lb", k), db, t, t_left)
        h_copy(("rb", k), db, t, t_right)
        h_copy(("la", k), da, t, t_left)
        h_copy(("so", k), pl.ds(sa.start, 2 * (sa.stop - sa.start)), t, t_sib)
        dp_col = jnp.concatenate([dprob_parts[(k, sa.start)], dprob_parts[(k, sb.start)]], axis=0)
        for i in range(n):
            p = p0 + i
            row = jnp.sum(eye * dp_col[i * CAP : (i + 1) * CAP, :], axis=0, keepdims=True)
            dps[p] = jnp.broadcast_to(row, (8, 128))
            o = ORDER[p]
            if o != 0:
                cp.add(("dp", o), dps.at[p], dpr.at[place(-o)], {"dp": (z + o) % 8})
        for i in range(n):
            s = slice((p0 + i) * CAP, (p0 + i + 1) * CAP)
            sc[s, :] = (pcol[s, :] * gr[s, :].astype(F32)).astype(BF16)

    dprob_parts = {}

    def stage_g1(k):
        sa, sb, da, db = halves(k)
        full = pl.ds(sa.start, 2 * (sa.stop - sa.start))
        cp.got(("ra", k))
        h_copy(("xa", k), da, t_left, t_right)
        cp.got(("lb", k))
        h_copy(("xb", k), db, t_right, t_left)
        cp.got(("rb", k))
        h_copy(("sl", k), full, t_left, t_sib)
        cp.got(("la", k))
        h_copy(("sr", k), full, t_right, t_sib)

    def stage_g2(k):
        sa, sb, da, db = halves(k)
        full = pl.ds(sa.start, 2 * (sa.stop - sa.start))
        cp.got(("xa", k))
        cp.got(("xb", k))
        h_copy(("sx", k), full, across * 2 + c, t_sib)

    def stage_x(k):
        p0, n = CHUNKS[k]
        r0, r = p0 * CAP, n * CAP
        for q in ("so", "sl", "sr", "sx"):
            cp.got((q, k))
        a = hh[1, r0 : r0 + r, :]
        b = hh[2, r0 : r0 + r, :]

        @pl.loop(0, 3)
        def _(n):
            cols = pl.ds(pl.multiple_of(n * 256, 256), 256)
            v = dot_nt(a, gw[cols, :]) + dot_nt(b, uw[cols, :])
            if ORDER[p0] == 0:
                dxo[:, cols] = v[0:CAP]
            dxs[r0 : r0 + r, cols] = v.astype(BF16)

        for p in range(p0, p0 + n):
            o = ORDER[p]
            if o != 0:
                cp.add(("dx", o), dxs.at[rows_of(p)], dxr.at[rows_of(place(-o))],
                       {"dp": (z + o) % 8})

    run = {"F": stage_f, "R1": stage_r1, "R2": stage_r2, "E": stage_e,
           "G1": stage_g1, "G2": stage_g2, "X": stage_x}
    steps = plan()
    last_f = max(i for i, (s, _) in enumerate(steps) if s == "F")
    for i, (s, k) in enumerate(steps):
        if s == "R1" and k == 0:
            probabilities()
        run[s](k)
        if i == last_f:
            @pl.loop(0, 3)
            def _(n):
                cols = pl.ds(pl.multiple_of(n * 256, 256), 256)
                tkt[cols, :] = tk[:, cols].T

    @pl.loop(0, 4)
    def _(n):
        cols = pl.ds(pl.multiple_of(n * 256, 256), 256)
        h0t[cols, :] = hh[0, :, cols].T

    @pl.loop(0, 3)
    def _(i):
        rows = pl.ds(pl.multiple_of(i * 256, 256), 256)
        lhs = tkt[rows, :]

        @pl.loop(0, 4)
        def _(n):
            cols = pl.ds(pl.multiple_of(n * 256, 256), 256)
            wout[0, rows, cols] = dot_nn(lhs, hh[1, :, cols]).astype(BF16)
            wout[1, rows, cols] = dot_nn(lhs, hh[2, :, cols]).astype(BF16)

    outs = [pltpu.make_async_copy(wout.at[0], gg_h, osem.at[0]),
            pltpu.make_async_copy(wout.at[1], ug_h, osem.at[1]),
            pltpu.make_async_copy(dw, dg_h, osem.at[2])]
    outs[0].start()
    outs[1].start()

    @pl.loop(0, 4)
    def _(i):
        rows = pl.ds(pl.multiple_of(i * 256, 256), 256)
        lhs = h0t[rows, :]

        @pl.loop(0, 3)
        def _(n):
            cols = pl.ds(pl.multiple_of(n * 256, 256), 256)
            dw[rows, cols] = dot_nn(lhs, sc[:, cols]).astype(BF16)

    outs[2].start()

    total = dxo[...]
    prob = dps[0]
    for p in range(8):
        o = ORDER[p]
        if o != 0:
            cp.got(("dp", -o if o != 4 else 4))
            prob = prob + dpr[p]
            cp.got(("dx", -o if o != 4 else 4))
            total = total + dxr[p * CAP : (p + 1) * CAP, :].astype(F32)
    rowdx[...] = total
    rowprob[...] = prob
    for o in outs:
        o.wait()
    cp.drain()


def mega(tokens, out_grad, rwt, idx, gate_w, up_w, down_w):
    vm = pl.BlockSpec(memory_space=pltpu.VMEM)
    hbm = pl.BlockSpec(memory_space=pl.ANY)
    V = pltpu.VMEM
    return pl.pallas_call(
        kernel,
        name="moe_backward",
        in_specs=[vm] * 4 + [hbm] * 3,
        out_specs=[hbm] * 3 + [vm] * 3,
        out_shape=[
            jax.ShapeDtypeStruct((768, 1024), BF16),
            jax.ShapeDtypeStruct((768, 1024), BF16),
            jax.ShapeDtypeStruct((1024, 768), BF16),
            jax.ShapeDtypeStruct((CAP, 768), F32),
            jax.ShapeDtypeStruct((8, 128), F32),
            jax.ShapeDtypeStruct((2, 128), F32),
        ],
        scratch_shapes=[
            V((768, 768), BF16), V((768, 768), BF16), V((768, 768), BF16), V((768, 768), BF16),
            V((768, 1024), BF16), V((768, 1024), BF16), V((1024, 768), BF16),
            V((2, 4, 768, 384), BF16), V((4, 768, 384), BF16),
            V((768, 384), BF16), V((768, 384), BF16), V((768, 384), BF16), V((768, 384), BF16),
            V((3, 768, 1024), BF16), V((1024, 768), BF16), V((768, 1), F32),
            V((8, 128), F32), V((8, 8, 128), F32), V((8, 128), F32), V((8, 8, 128), F32),
            V((8, 8, 128), F32), V((8, 8, 128), F32),
            V((768, 768), BF16), V((768, 768), BF16), V((CAP, 768), F32),
            V((2, 768, 1024), BF16),
            pltpu.SemaphoreType.DMA((N_COPIES,)), pltpu.SemaphoreType.DMA((N_COPIES,)),
            pltpu.SemaphoreType.DMA((3,)), pltpu.SemaphoreType.DMA((3,)),
        ],
        compiler_params=pltpu.CompilerParams(
            collective_id=0, has_side_effects=True, vmem_limit_bytes=56 * 1024 * 1024
        ),
    )(tokens, out_grad, rwt, idx, gate_w, up_w, down_w)


def from_everyone(array, axis):
    count = lax.axis_size(axis)
    return lax.all_to_all(
        jnp.broadcast_to(array[None], (count, *array.shape)), axis, 0, 0, tiled=True
    )


def of_everyone(array, axis):
    return from_everyone(array, axis).sum(axis=0)


def split_up(array, dim, count):
    before, after = (array.shape[:dim], array.shape[dim + 1 :])
    return jnp.moveaxis(array.reshape(*before, count, -1, *after), dim, 0)


def sent_and_summed(array, axis, dim):
    parts = split_up(array, dim, lax.axis_size(axis))
    arrived = lax.all_to_all(parts, axis, split_axis=0, concat_axis=0, tiled=True)
    return arrived.astype(jnp.float32).sum(axis=0)


def in_one_piece_2(arrays, axis, dim, along):
    both = jnp.concatenate(arrays, axis=along)
    filled, at, gathered = (sent_and_summed(both, axis, dim), 0, [])
    for a in arrays:
        gathered.append(lax.slice_in_dim(filled, at, at + a.shape[along], axis=along))
        at += a.shape[along]
    return tuple(gathered)


def split_parts(values):
    high_part = values.astype(jnp.bfloat16)
    low_part = (values - high_part.astype(jnp.float32)).astype(jnp.bfloat16)
    return (high_part, low_part)


def table_apply(form, table_low, values):
    high_part, low_part = split_parts(values)
    return jnp.einsum(form, table_low, high_part, preferred_element_type=jnp.float32) + jnp.einsum(
        form, table_low, low_part, preferred_element_type=jnp.float32
    )


def slot_table(experts_here, slots_here, expert_id, capacity):
    positions = lax.broadcasted_iota(jnp.int32, (capacity, experts_here.shape[0]), 0)
    first_table = (experts_here[:, 0] == expert_id)[None, :] & (
        slots_here[:, 0][None, :] == positions
    )
    second_table = (experts_here[:, 1] == expert_id)[None, :] & (
        slots_here[:, 1][None, :] == positions
    )
    return (first_table.astype(jnp.float32), second_table.astype(jnp.float32))


def shards(
    tokens, out_grad, router_weight, gate_weight, up_weight, down_weight, expert_index, slot_index
):
    expert_count = router_weight.shape[1]
    expert_id = lax.axis_index("expert")
    rwt = jnp.concatenate([router_weight.T, jnp.zeros((4, router_weight.shape[0]), BF16)], axis=0)
    idx = jnp.concatenate([expert_index, slot_index], axis=1).T
    gate_grad, up_grad, down_grad, row_dx, prob8, picks = mega(
        tokens, out_grad, rwt, idx, gate_weight[0], up_weight[0], down_weight[0]
    )
    row_prob = prob8[0, :CAP]
    pick_prob = picks.T
    first_table, second_table = slot_table(expert_index, slot_index, expert_id, CAP)
    select_low = (first_table + second_table).astype(jnp.bfloat16)
    own_expert = (lax.broadcasted_iota(jnp.int32, (1, expert_count), 1) == expert_id).astype(
        jnp.float32
    )
    token_dx = table_apply("cn,cd->nd", select_low, row_dx)
    token_prob = table_apply("cn,c->n", select_low, row_prob)
    token_term, prob_rows = in_one_piece_2(
        (token_dx.astype(jnp.bfloat16), (token_prob[:, None] * own_expert).astype(jnp.bfloat16)),
        "expert",
        0,
        1,
    )
    prob_rows = of_everyone(prob_rows, "tensor")
    quarter = token_term.shape[0]
    offset = expert_id * quarter
    part_prob = lax.dynamic_slice_in_dim(pick_prob, offset, quarter, 0)
    part_experts = lax.dynamic_slice_in_dim(expert_index, offset, quarter, 0)
    part_tokens = lax.dynamic_slice_in_dim(tokens, offset, quarter, 0)
    pick_grad = jnp.take_along_axis(prob_rows, part_experts, axis=1)
    mixed_grad = jnp.sum(part_prob * pick_grad, axis=1, keepdims=True)
    weights = part_prob * (pick_grad - mixed_grad)
    onehot = (
        part_experts[:, :, None] == lax.broadcasted_iota(jnp.int32, (1, 1, expert_count), 2)
    ).astype(jnp.float32)
    logit_grad = jnp.sum(onehot * weights[:, :, None], axis=1)
    router_rows = router_weight.astype(jnp.float32)
    tokens_grad = (token_term + jnp.dot(logit_grad, router_rows.T)).astype(jnp.bfloat16)
    router_part = jnp.dot(part_tokens.astype(jnp.float32).T, logit_grad)
    router_grad = of_everyone(router_part, ("dp", "expert"))
    return (tokens_grad, router_grad, gate_grad[None], up_grad[None], down_grad[None])


def solution(mesh):
    in_specs = (
        P("dp", "tensor"),
        P("dp", "tensor"),
        P("tensor", None),
        P("expert", "tensor", "dp"),
        P("expert", "tensor", "dp"),
        P("expert", "dp", "tensor"),
        P("dp", None),
        P("dp", None),
    )
    out_specs = (
        P(("dp", "expert"), "tensor"),
        P("tensor", None),
        P("expert", "tensor", "dp"),
        P("expert", "tensor", "dp"),
        P("expert", "dp", "tensor"),
    )
    return jax.shard_map(shards, mesh=mesh, in_specs=in_specs, out_specs=out_specs, check_vma=False)
```

time: 259 us -> 153 us (0.59)
  waiting for transfers between devices: 164 us -> 23.7 us
  Pallas kernels: 0 us -> 90.4 us
  matrix products: 31.1 us -> 5.99 us
  between operations: 14 us -> 0.74 us
  starting transfers between devices: 26.4 us -> 15.6 us
  other arithmetic: 12 us -> 4.48 us
    pallas_call x0 -> x1, Pallas kernels: none -> 90.4 us  [mega(): pl.pallas_call(kernel, name='moe_backward', in_specs=[vm] * 4 + [hbm] * 3...]
    all_gather x2 -> x0, waiting for transfers between devices: 79.4 us -> none  [the longest x1 40.8 us: sent_together(): lax.all_gather(both, axis, axis=dim, tiled=True)]
    reduce_scatter x1 -> x0, waiting for transfers between devices: 39.9 us -> none  [side_by_side(): lax.psum_scatter(both, axis, scatter_dimension=dim, tiled=True)]
    all_to_all x2 -> x1, waiting for transfers between devices: 40.3 us -> 6.46 us  [sent_and_summed(): lax.all_to_all(parts, axis, split_axis=0, concat_axis=0, tiled=True)]
    dot_general x13 -> x0, matrix products: 28.5 us -> none  [the longest x3 12.9 us: contract_rows(): lax.dot_general(left_side, right_side, (((0,), (0,)), ((), ())), preferre...]
    all_to_all x3 -> x2, waiting for transfers between devices: 4.54 us -> 17.2 us  [from_everyone(): lax.all_to_all(jnp.broadcast_to(array[None], (count, *array.shape)), axis...]
    all_to_all x2 -> x1, starting transfers between devices: 10.7 us -> 4.27 us  [sent_and_summed(): lax.all_to_all(parts, axis, split_axis=0, concat_axis=0, tiled=True)]
    concatenate x4 -> x0, other arithmetic: 5.12 us -> none  [the longest x1 2.3 us: side_by_side(): both = jnp.concatenate(arrays, axis=along)]
  transfers between devices with their start and end apart: 8 -> 3, of which waited for: 7 -> 3; matrix products, arithmetic and copies ran while one was open for 8% -> 1% of each run, Pallas kernels for 0% -> 0%
where the time goes in v1:
time: 153 us; the launch traced here: 152 us
  Pallas kernels  90.4 us (59%)
  waiting for transfers between devices  23.7 us (15%)
  starting transfers between devices  15.6 us (10%)
  local copies, waits for them, and re-layouts  10.7 us (7%)
  matrix products  5.99 us (4%)
  other arithmetic  4.48 us (3%)
    pallas_call x1, Pallas kernels, mega(): pl.pallas_call(kernel, name='moe_backward', in_specs=[vm] * 4 + [hbm] * 3...  90.4 us
    all_to_all x2, waiting for transfers between devices, from_everyone(): lax.all_to_all(jnp.broadcast_to(array[None], (count, *array.shape)), axis...  17.2 us
    all_to_all x2, starting transfers between devices, from_everyone(): lax.all_to_all(jnp.broadcast_to(array[None], (count, *array.shape)), axis...  11.4 us
    all_to_all x1, waiting for transfers between devices, sent_and_summed(): lax.all_to_all(parts, axis, split_axis=0, concat_axis=0, tiled=True)  6.46 us
    unnamed x18, local copies, waits for them, and re-layouts  5.89 us
    all_to_all x1, starting transfers between devices, sent_and_summed(): lax.all_to_all(parts, axis, split_axis=0, concat_axis=0, tiled=True)  4.27 us
  transfers between devices with their start and end apart: 3, of which 3 were waited for; matrix products, arithmetic and copies ran while one was open for 1% of the time, Pallas kernels for 0%

profile of v1, /device:TPU:1, one launch (start us, length us, event | category | flops | bytes accessed | tf_op | source)
XLA Modules:
  0.0 151.7 jit_solution(11627331321783226712)
XLA Ops:
  0.6 0.8 slice_bitcast_fusion.1
  1.4 1.3 add_bitcast_fusion.idx
  2.7 0.8 compare_bitcast_fusion.1
  3.4 1.3 concatenate.9.rwt
  4.7 90.4 %moe_backward.1 = (bf16[768,1024]{1,0:T(8,128)(2,1)}, bf16[768,1024]{1,0:T(8,128)(2,1)}, bf16[1024,768]{1,0:T(8,128)(2,1)}, f32[96,768]{1,0:T(8,128)}, f32[8,128]{1,0:T(8,128)}, /*index=5*/f32[2,128]{1,0:T(2,128)}) custom-call(bf16[128,768]{1,0:T(8,128)(2,1)} %tok_in.1, bf16[128,768]{1,0:T(8,128)(2,1)} %og_in.1, bf16[8,768]{1,0:T(8,128)(2,1)} %concatenate.9.rwt, ...), custom_call_target="tpu_custom_call" | custom-call | tf_op jit(solution)/shard_map/moe_backward/pallas_call | solution.py:420
  95.2 0.0 copy-start.4
  95.2 0.8 convolution_bitcast_fusion.1
  96.0 0.8 fusion.2
  96.8 0.1 multiply_convert_fusion
  96.9 0.1 copy.42
  97.0 1.2 fusion.4
  98.3 1.3 fusion
  99.6 0.7 pad_maximum_fusion
  100.3 4.3 %all-to-all-start = ((bf16[4,32,772]{2,1,0:T(8,128)(2,1)}), bf16[4,32,772]{2,1,0:T(8,128)(2,1)S(1)}, u32[]{:S(2)}, u32[]{:S(2)}) async-start(bf16[4,32,772]{2,1,0:T(8,128)(2,1)} %bitcast.14), calls=%async_computation | async-start | bytes 458752 | tf_op jit(solution)/shard_map/all_to_all | solution.py:470
  104.5 6.5 %all-to-all-done = bf16[4,32,772]{2,1,0:T(8,128)(2,1)S(1)} async-done(((bf16[4,32,772]{2,1,0:T(8,128)(2,1)}), bf16[4,32,772]{2,1,0:T(8,128)(2,1)S(1)}, u32[]{:S(2)}, u32[]{:S(2)}) %all-to-all-start) | async-done | bytes 197664 | tf_op jit(solution)/shard_map/all_to_all | solution.py:470
  111.1 0.1 copy.43
  111.1 0.7 reshape.68
  111.8 5.5 %all-to-all-start.1 = ((f32[8,1,128]{2,1,0:T(1,128)}), f32[8,1,128]{2,1,0:T(1,128)S(1)}, u32[]{:S(2)}, u32[]{:S(2)}) async-start(f32[8,1,128]{2,1,0:T(1,128)} %reshape.68), calls=%async_computation.1 | async-start | bytes 8192 | tf_op jit(solution)/shard_map/all_to_all | solution.py:454
  117.3 0.0 copy-done.4
  117.3 0.1 bitcast_or_fusion
  117.4 0.1 copy.44
  117.5 0.1 reshape.53
  117.6 4.2 %all-to-all-done.1 = f32[8,1,128]{2,1,0:T(1,128)S(1)} async-done(((f32[8,1,128]{2,1,0:T(1,128)}), f32[8,1,128]{2,1,0:T(1,128)S(1)}, u32[]{:S(2)}, u32[]{:S(2)}) %all-to-all-start.1) | async-done | bytes 4128 | tf_op jit(solution)/shard_map/all_to_all | solution.py:454
  121.9 0.5 broadcast.53
  122.4 0.7 reduce
  123.1 0.1 reshape.69
  123.2 0.0 copy-start.3
  123.2 0.9 gather_fusion
  124.1 0.0 copy-start.2
  124.1 0.1 reshape.56
  124.2 0.1 copy.45
  124.2 0.0 copy-done.5
  124.2 0.1 fusion.10
  124.3 0.1 bitcast_multiply_fusion
  124.4 1.0 fusion.6
  125.4 0.8 broadcast_in_dim.16
  126.2 5.9 %all-to-all-start.2 = ((f32[32,768,4]{1,2,0:T(4,128)}), f32[32,768,4]{1,2,0:T(4,128)S(1)}, u32[]{:S(2)}, u32[]{:S(2)}) async-start(f32[32,768,4]{1,2,0:T(4,128)} %broadcast_in_dim.16), calls=%async_computation.2 | async-start | bytes 786432 | tf_op jit(solution)/shard_map/all_to_all | solution.py:454
  132.1 0.0 copy-done.3
  132.1 0.8 fusion.1
  132.9 13.0 %all-to-all-done.2 = f32[32,768,4]{1,2,0:T(4,128)S(1)} async-done(((f32[32,768,4]{1,2,0:T(4,128)}), f32[32,768,4]{1,2,0:T(4,128)S(1)}, u32[]{:S(2)}, u32[]{:S(2)}) %all-to-all-start.2) | async-done | bytes 393248 | tf_op jit(solution)/shard_map/all_to_all | solution.py:454
  145.9 0.7 reduce_sum.49
  146.6 0.0 copy-done.2
  146.6 0.0 copy-start.1
  146.6 1.1 copy.49
  147.8 0.8 copy-done.1
  148.6 1.1 copy.50
  149.7 0.8 copy-done
  150.6 1.1 copy.51
  (8 shorter events, 0.1 us)
Async XLA Ops:
  95.2 22.2 %copy-start.4 = (s32[128,2]{0,1:T(2,128)S(1)}, s32[128,2]{0,1:T(2,128)}, u32[]{:S(2)}) copy-start(s32[128,2]{0,1:T(2,128)} %param.14) | copy-start | bytes 3076
  100.3 10.7 %all-to-all-start = ((bf16[4,32,772]{2,1,0:T(8,128)(2,1)}), bf16[4,32,772]{2,1,0:T(8,128)(2,1)S(1)}, u32[]{:S(2)}, u32[]{:S(2)}) async-start(bf16[4,32,772]{2,1,0:T(8,128)(2,1)} %bitcast.14), calls=%async_computation | async-start | bytes 458752 | tf_op jit(solution)/shard_map/all_to_all | solution.py:470
  111.8 10.0 %all-to-all-start.1 = ((f32[8,1,128]{2,1,0:T(1,128)}), f32[8,1,128]{2,1,0:T(1,128)S(1)}, u32[]{:S(2)}, u32[]{:S(2)}) async-start(f32[8,1,128]{2,1,0:T(1,128)} %reshape.68), calls=%async_computation.1 | async-start | bytes 8192 | tf_op jit(solution)/shard_map/all_to_all | solution.py:454
  123.2 1.1 copy-start.5
  123.2 9.0 %copy-start.3 = (bf16[768,4]{0,1:T(4,128)(2,1)S(1)}, bf16[768,4]{0,1:T(4,128)(2,1)}, u32[]{:S(2)}) copy-start(bf16[768,4]{0,1:T(4,128)(2,1)} %param.10) | copy-start | bytes 18436
  124.1 22.6 %copy-start.2 = (bf16[768,1024]{1,0:T(8,128)(2,1)S(1)}, bf16[768,1024]{1,0:T(8,128)(2,1)}, u32[]{:S(2)}) copy-start(bf16[768,1024]{1,0:T(8,128)(2,1)} %get-tuple-element.14) | copy-start | bytes 4718596
  126.2 19.7 %all-to-all-start.2 = ((f32[32,768,4]{1,2,0:T(4,128)}), f32[32,768,4]{1,2,0:T(4,128)S(1)}, u32[]{:S(2)}, u32[]{:S(2)}) async-start(f32[32,768,4]{1,2,0:T(4,128)} %broadcast_in_dim.16), calls=%async_computation.2 | async-start | bytes 786432 | tf_op jit(solution)/shard_map/all_to_all | solution.py:454
  146.6 2.0 %copy-start.1 = (bf16[768,1024]{1,0:T(8,128)(2,1)S(1)}, bf16[768,1024]{1,0:T(8,128)(2,1)}, u32[]{:S(2)}) copy-start(bf16[768,1024]{1,0:T(8,128)(2,1)} %get-tuple-element.15) | copy-start | bytes 4718596
  148.6 2.0 %copy-start = (bf16[1024,768]{1,0:T(8,128)(2,1)S(1)}, bf16[1024,768]{1,0:T(8,128)(2,1)}, u32[]{:S(2)}) copy-start(bf16[1024,768]{1,0:T(8,128)(2,1)} %get-tuple-element.16) | copy-start | bytes 4718596

commit v2 on v1

--- a/solution.py
+++ b/solution.py
@@ -27,7 +27,7 @@
     _at += _n
 
 STAGES = ("F", "R1", "R2", "E", "G1", "G2", "X")
-SKEW = 2
+SKEW = 1
 
 
 def plan():
@@ -79,10 +79,11 @@
 
 
 def kernel(
-    tok_in, og_in, rwt, idx, gw_h, uw_h, dw_h,
-    gg_h, ug_h, dg_h, rowdx, rowprob, picks,
+    tok_in, og_in, rwt, ex, sl, gw_h, uw_h, dw_h,
+    tok_out, router_out, gg_h, ug_h, dg_h,
     tk, gr, sc, tkt, gw, uw, dw, part, dbuf, fa, fb, rl, rr, hh, h0t, pcol,
     lgs, lgr, prs, prr, dps, dpr, dxs, dxr, dxo, wout,
+    pts, ptr, pys, pyr, ws, wr, rgs, rgr, yd, yr, lg3,
     send_sem, recv_sem, wsem, osem,
 ):
     z = lax.axis_index("dp")
@@ -105,14 +106,16 @@
     for k in range(1, 8):
         pl.semaphore_signal(barrier, inc=1, device_id={"dp": (z + k) % 8}, device_id_type=MESH)
         pl.semaphore_signal(barrier, inc=1, device_id={"tensor": (t + k) % 8}, device_id_type=MESH)
-    pl.semaphore_wait(barrier, 14)
+    for k in range(1, 4):
+        pl.semaphore_signal(barrier, inc=1, device_id={"expert": (y + k) % 4}, device_id_type=MESH)
+    pl.semaphore_wait(barrier, 17)
 
     cp = Copies(send_sem, recv_sem)
 
     slot_at = lax.broadcasted_iota(jnp.int32, (CAP, 128), 0)
     lane_at = lax.broadcasted_iota(jnp.int32, (CAP, 128), 1)
     eye = (slot_at == lane_at).astype(F32)
-    e0, e1, s0, s1 = idx[0:1, :], idx[1:2, :], idx[2:3, :], idx[3:4, :]
+    e0, e1, s0, s1 = ex[0:1, :], ex[1:2, :], sl[0:1, :], sl[1:2, :]
     table0 = jnp.where((e0 == y) & (s0 == slot_at), 1.0, 0.0).astype(F32)
     table1 = jnp.where((e1 == y) & (s1 == slot_at), 1.0, 0.0).astype(F32)
     select = (table0 + table1).astype(BF16)
@@ -137,15 +140,18 @@
         ring(0, which)
         ring_back(0, which)
 
-    lgs[...] = dot_nt(rwt[...], tok_in[...])
+    lgs[4:8, :] = jnp.zeros((4, 128), F32)
+    lgs[0:4, :] = dot_nt(rwt[...], tok_in[...])
     for k in range(1, 8):
         cp.add(("lg", k), lgs, lgr.at[k], {"tensor": (t + k) % 8})
 
+    picks = []
+
     def probabilities():
-        total = lgs[...]
+        total = lgs[0:4, :]
         for k in range(1, 8):
             cp.got(("lg", k))
-            total = total + lgr[k]
+            total = total + lgr[k][0:4, :]
         l0 = jnp.zeros((1, 128), F32)
         l1 = jnp.zeros((1, 128), F32)
         for j in range(4):
@@ -153,8 +159,7 @@
             l1 = l1 + jnp.where(e1 == j, total[j : j + 1, :], 0.0)
         p0 = jax.nn.sigmoid(l0 - l1)
         p1 = jax.nn.sigmoid(l1 - l0)
-        picks[0:1, :] = p0
-        picks[1:2, :] = p1
+        picks.extend((p0, p1))
         low0 = p0.astype(BF16).astype(F32)
         low1 = p1.astype(BF16).astype(F32)
         col = jnp.sum(table0 * low0 + table1 * low1, axis=1, keepdims=True)
@@ -349,204 +354,231 @@
                 cp.add(("dx", o), dxs.at[rows_of(p)], dxr.at[rows_of(place(-o))],
                        {"dp": (z + o) % 8})
 
+    def to_col(row):
+        return jnp.sum(eye * row, axis=1, keepdims=True)
+
+    def to_row(col):
+        return jnp.sum(eye * col, axis=0, keepdims=True)
+
+    def parts3(v):
+        hi = v.astype(BF16)
+        rest = v - hi.astype(F32)
+        mid = rest.astype(BF16)
+        low = (rest - mid.astype(F32)).astype(BF16)
+        return hi, mid, low
+
+    def pair8(r0, r1):
+        row = lax.broadcasted_iota(jnp.int32, (8, 128), 0)
+        return jnp.where(row == 0, r0, jnp.where(row == 1, r1, 0.0))
+
+    def router_1():
+        total = dps[0][0:1, :]
+        for p in range(8):
+            if ORDER[p] != 0:
+                o = ORDER[p]
+                cp.got(("dp", -o if o != 4 else 4))
+                total = total + dpr[p][0:1, :]
+        col = to_col(total)
+        pts[...] = pair8(jnp.sum(table0 * col, axis=0, keepdims=True),
+                         jnp.sum(table1 * col, axis=0, keepdims=True))
+        for k in range(1, 8):
+            cp.add(("pt", k), pts, ptr.at[k], {"tensor": (t + k) % 8})
+
+    def router_2():
+        total = pts[...]
+        for k in range(1, 8):
+            cp.got(("pt", k))
+            total = total + ptr[k]
+        pys[...] = total
+        for k in range(1, 4):
+            cp.add(("py", k), pys, pyr.at[k], {"expert": (y + k) % 4})
+
+    def router_3():
+        total = pys[...]
+        for k in range(1, 4):
+            cp.got(("py", k))
+            total = total + pyr[k]
+        d0, d1 = total[0:1, :], total[1:2, :]
+        p0, p1 = picks
+        mixed = p0 * d0 + p1 * d1
+        w0 = p0 * (d0 - mixed)
+        w1 = p1 * (d1 - mixed)
+        ws[...] = jnp.broadcast_to(
+            to_row(jnp.sum(table0 * w0 + table1 * w1, axis=1, keepdims=True)), (8, 128))
+        for k in range(1, 8):
+            cp.add(("w", k), ws, wr.at[place(-k)], {"dp": (z + k) % 8})
+        i0 = lax.broadcasted_iota(jnp.int32, (128, 128), 0)
+        i1 = lax.broadcasted_iota(jnp.int32, (128, 128), 1)
+        eye_t = (i0 == i1).astype(F32)
+
+        def col_t(row):
+            return jnp.sum(eye_t * row, axis=1, keepdims=True)
+
+        lane = lax.broadcasted_iota(jnp.int32, (128, 16), 1)
+        of_expert = (lane % 4).astype(F32)
+        v = (jnp.where(col_t(e0.astype(F32)) == of_expert, col_t(w0), 0.0)
+             + jnp.where(col_t(e1.astype(F32)) == of_expert, col_t(w1), 0.0))
+        hi, mid, low = (q.astype(F32) for q in parts3(v))
+        lg3[...] = jnp.where(lane < 4, hi, jnp.where(lane < 8, mid, jnp.where(lane < 12, low, 0.0)))
+
+    def router_4():
+        acc = jnp.zeros((8, 768), F32)
+        row = lax.broadcasted_iota(jnp.int32, (8, 128), 0)
+        for p in range(8):
+            if ORDER[p] == 0:
+                v = ws[...]
+            else:
+                cp.got(("w", (-ORDER[p]) % 8))
+                v = wr[p]
+            hi, mid, low = (q.astype(F32) for q in parts3(v))
+            lhs = jnp.where(row == 0, hi, jnp.where(row == 1, mid, jnp.where(row == 2, low, 0.0)))
+            acc = acc + dot_nn(lhs[:, 0:CAP].astype(BF16), tk[p * CAP : (p + 1) * CAP, :])
+        rgs[...] = jnp.broadcast_to(jnp.sum(acc, axis=0, keepdims=True), (8, 768))
+        rgr[0] = rgs[...]
+        for k in range(1, 4):
+            cp.add(("rg", k), rgs, rgr.at[k], {"expert": (y + k) % 4})
+
+    def router_5():
+        for k in range(1, 4):
+            cp.got(("rg", k))
+        for j in range(4):
+            k = (y + 4 - j) % 4
+            router_out[j : j + 1, :] = rgr[k][0:1, :]
+
+    def tokens_1():
+        total = dxo[...]
+        for p in range(8):
+            o = ORDER[p]
+            if o != 0:
+                cp.got(("dx", -o if o != 4 else 4))
+                total = total + dxr[p * CAP : (p + 1) * CAP, :].astype(F32)
+        hi = total.astype(BF16)
+        low = (total - hi.astype(F32)).astype(BF16)
+        both = jnp.concatenate([hi, low], axis=0)
+        pick = jnp.concatenate([select.astype(F32).T.astype(BF16)] * 2, axis=1)
+        v = dot_nn(pick, both)
+        yd[...] = v.astype(BF16)
+        for k in range(1, 4):
+            rows = pl.ds(pl.multiple_of(((y + k) % 4) * 32, 32), 32)
+            cp.add(("yd", k), yd.at[rows, :], yr.at[k], {"expert": (y + k) % 4})
+
+    def tokens_2():
+        rows = pl.ds(pl.multiple_of(y * 32, 32), 32)
+        total = yd[rows, :].astype(F32)
+        total = total + dot_nn(lg3[rows, :].astype(BF16), jnp.concatenate([rwt[...]] * 4, axis=0))
+        for k in range(1, 4):
+            cp.got(("yd", k))
+            total = total + yr[k].astype(F32)
+        tok_out[...] = total.astype(BF16)
+
+    def fill_1():
+        @pl.loop(0, 3)
+        def _(n):
+            cols = pl.ds(pl.multiple_of(n * 256, 256), 256)
+            tkt[cols, :] = tk[:, cols].T
+
+    outs = [pltpu.make_async_copy(wout.at[0], gg_h, osem.at[0]),
+            pltpu.make_async_copy(wout.at[1], ug_h, osem.at[1]),
+            pltpu.make_async_copy(dw, dg_h, osem.at[2])]
+
+    def weights_1():
+        @pl.loop(0, 3)
+        def _(i):
+            rows = pl.ds(pl.multiple_of(i * 256, 256), 256)
+            lhs = tkt[rows, :]
+
+            @pl.loop(0, 4)
+            def _(n):
+                cols = pl.ds(pl.multiple_of(n * 256, 256), 256)
+                wout[0, rows, cols] = dot_nn(lhs, hh[1, :, cols]).astype(BF16)
+                wout[1, rows, cols] = dot_nn(lhs, hh[2, :, cols]).astype(BF16)
+
+        outs[0].start()
+        outs[1].start()
+
+    def weights_2():
+        @pl.loop(0, 4)
+        def _(i):
+            rows = pl.ds(pl.multiple_of(i * 256, 256), 256)
+            h0t[...] = hh[0, :, rows].T
+
+            @pl.loop(0, 3)
+            def _(n):
+                cols = pl.ds(pl.multiple_of(n * 256, 256), 256)
+                dw[rows, cols] = dot_nn(h0t[...], sc[:, cols]).astype(BF16)
+
+        outs[2].start()
+
     run = {"F": stage_f, "R1": stage_r1, "R2": stage_r2, "E": stage_e,
            "G1": stage_g1, "G2": stage_g2, "X": stage_x}
     steps = plan()
+    end = len(CHUNKS) - 1
     last_f = max(i for i, (s, _) in enumerate(steps) if s == "F")
     for i, (s, k) in enumerate(steps):
         if s == "R1" and k == 0:
             probabilities()
         run[s](k)
         if i == last_f:
-            @pl.loop(0, 3)
-            def _(n):
-                cols = pl.ds(pl.multiple_of(n * 256, 256), 256)
-                tkt[cols, :] = tk[:, cols].T
-
-    @pl.loop(0, 4)
-    def _(n):
-        cols = pl.ds(pl.multiple_of(n * 256, 256), 256)
-        h0t[cols, :] = hh[0, :, cols].T
-
-    @pl.loop(0, 3)
-    def _(i):
-        rows = pl.ds(pl.multiple_of(i * 256, 256), 256)
-        lhs = tkt[rows, :]
-
-        @pl.loop(0, 4)
-        def _(n):
-            cols = pl.ds(pl.multiple_of(n * 256, 256), 256)
-            wout[0, rows, cols] = dot_nn(lhs, hh[1, :, cols]).astype(BF16)
-            wout[1, rows, cols] = dot_nn(lhs, hh[2, :, cols]).astype(BF16)
-
-    outs = [pltpu.make_async_copy(wout.at[0], gg_h, osem.at[0]),
-            pltpu.make_async_copy(wout.at[1], ug_h, osem.at[1]),
-            pltpu.make_async_copy(dw, dg_h, osem.at[2])]
-    outs[0].start()
-    outs[1].start()
-
-    @pl.loop(0, 4)
-    def _(i):
-        rows = pl.ds(pl.multiple_of(i * 256, 256), 256)
-        lhs = h0t[rows, :]
-
-        @pl.loop(0, 3)
-        def _(n):
-            cols = pl.ds(pl.multiple_of(n * 256, 256), 256)
-            dw[rows, cols] = dot_nn(lhs, sc[:, cols]).astype(BF16)
-
-    outs[2].start()
-
-    total = dxo[...]
-    prob = dps[0]
-    for p in range(8):
-        o = ORDER[p]
-        if o != 0:
-            cp.got(("dp", -o if o != 4 else 4))
-            prob = prob + dpr[p]
-            cp.got(("dx", -o if o != 4 else 4))
-            total = total + dxr[p * CAP : (p + 1) * CAP, :].astype(F32)
-    rowdx[...] = total
-    rowprob[...] = prob
+            fill_1()
+        if (s, k) == ("G1", end):
+            router_1()
+        if (s, k) == ("G2", end):
+            router_2()
+    router_3()
+    weights_1()
+    router_4()
+    tokens_1()
+    weights_2()
+    router_5()
+    tokens_2()
     for o in outs:
         o.wait()
     cp.drain()
 
 
-def mega(tokens, out_grad, rwt, idx, gate_w, up_w, down_w):
+def shards(
+    tokens, out_grad, router_weight, gate_weight, up_weight, down_weight, expert_index, slot_index
+):
     vm = pl.BlockSpec(memory_space=pltpu.VMEM)
     hbm = pl.BlockSpec(memory_space=pl.ANY)
     V = pltpu.VMEM
-    return pl.pallas_call(
+    small = V((8, 128), F32)
+    several = V((8, 8, 128), F32)
+    tokens_grad, router_grad, gate_grad, up_grad, down_grad = pl.pallas_call(
         kernel,
         name="moe_backward",
-        in_specs=[vm] * 4 + [hbm] * 3,
-        out_specs=[hbm] * 3 + [vm] * 3,
+        in_specs=[vm] * 5 + [hbm] * 3,
+        out_specs=[vm] * 2 + [hbm] * 3,
         out_shape=[
+            jax.ShapeDtypeStruct((32, 768), BF16),
+            jax.ShapeDtypeStruct((4, 768), F32),
             jax.ShapeDtypeStruct((768, 1024), BF16),
             jax.ShapeDtypeStruct((768, 1024), BF16),
             jax.ShapeDtypeStruct((1024, 768), BF16),
-            jax.ShapeDtypeStruct((CAP, 768), F32),
-            jax.ShapeDtypeStruct((8, 128), F32),
-            jax.ShapeDtypeStruct((2, 128), F32),
         ],
         scratch_shapes=[
             V((768, 768), BF16), V((768, 768), BF16), V((768, 768), BF16), V((768, 768), BF16),
             V((768, 1024), BF16), V((768, 1024), BF16), V((1024, 768), BF16),
             V((2, 4, 768, 384), BF16), V((4, 768, 384), BF16),
             V((768, 384), BF16), V((768, 384), BF16), V((768, 384), BF16), V((768, 384), BF16),
-            V((3, 768, 1024), BF16), V((1024, 768), BF16), V((768, 1), F32),
-            V((8, 128), F32), V((8, 8, 128), F32), V((8, 128), F32), V((8, 8, 128), F32),
-            V((8, 8, 128), F32), V((8, 8, 128), F32),
+            V((3, 768, 1024), BF16), V((256, 768), BF16), V((768, 1), F32),
+            small, several, small, several, several, several,
             V((768, 768), BF16), V((768, 768), BF16), V((CAP, 768), F32),
             V((2, 768, 1024), BF16),
+            small, several, small, V((4, 8, 128), F32), small, several,
+            V((8, 768), F32), V((4, 8, 768), F32), V((128, 768), BF16), V((4, 32, 768), BF16),
+            V((128, 16), F32),
             pltpu.SemaphoreType.DMA((N_COPIES,)), pltpu.SemaphoreType.DMA((N_COPIES,)),
             pltpu.SemaphoreType.DMA((3,)), pltpu.SemaphoreType.DMA((3,)),
         ],
         compiler_params=pltpu.CompilerParams(
             collective_id=0, has_side_effects=True, vmem_limit_bytes=56 * 1024 * 1024
         ),
-    )(tokens, out_grad, rwt, idx, gate_w, up_w, down_w)
-
-
-def from_everyone(array, axis):
-    count = lax.axis_size(axis)
-    return lax.all_to_all(
-        jnp.broadcast_to(array[None], (count, *array.shape)), axis, 0, 0, tiled=True
+    )(
+        tokens, out_grad, router_weight.T, expert_index.T, slot_index.T,
+        gate_weight[0], up_weight[0], down_weight[0],
     )
-
-
-def of_everyone(array, axis):
-    return from_everyone(array, axis).sum(axis=0)
-
-
-def split_up(array, dim, count):
-    before, after = (array.shape[:dim], array.shape[dim + 1 :])
-    return jnp.moveaxis(array.reshape(*before, count, -1, *after), dim, 0)
-
-
-def sent_and_summed(array, axis, dim):
-    parts = split_up(array, dim, lax.axis_size(axis))
-    arrived = lax.all_to_all(parts, axis, split_axis=0, concat_axis=0, tiled=True)
-    return arrived.astype(jnp.float32).sum(axis=0)
-
-
-def in_one_piece_2(arrays, axis, dim, along):
-    both = jnp.concatenate(arrays, axis=along)
-    filled, at, gathered = (sent_and_summed(both, axis, dim), 0, [])
-    for a in arrays:
-        gathered.append(lax.slice_in_dim(filled, at, at + a.shape[along], axis=along))
-        at += a.shape[along]
-    return tuple(gathered)
-
-
-def split_parts(values):
-    high_part = values.astype(jnp.bfloat16)
-    low_part = (values - high_part.astype(jnp.float32)).astype(jnp.bfloat16)
-    return (high_part, low_part)
-
-
-def table_apply(form, table_low, values):
-    high_part, low_part = split_parts(values)
-    return jnp.einsum(form, table_low, high_part, preferred_element_type=jnp.float32) + jnp.einsum(
-        form, table_low, low_part, preferred_element_type=jnp.float32
-    )
-
-
-def slot_table(experts_here, slots_here, expert_id, capacity):
-    positions = lax.broadcasted_iota(jnp.int32, (capacity, experts_here.shape[0]), 0)
-    first_table = (experts_here[:, 0] == expert_id)[None, :] & (
-        slots_here[:, 0][None, :] == positions
-    )
-    second_table = (experts_here[:, 1] == expert_id)[None, :] & (
-        slots_here[:, 1][None, :] == positions
-    )
-    return (first_table.astype(jnp.float32), second_table.astype(jnp.float32))
-
-
-def shards(
-    tokens, out_grad, router_weight, gate_weight, up_weight, down_weight, expert_index, slot_index
-):
-    expert_count = router_weight.shape[1]
-    expert_id = lax.axis_index("expert")
-    rwt = jnp.concatenate([router_weight.T, jnp.zeros((4, router_weight.shape[0]), BF16)], axis=0)
-    idx = jnp.concatenate([expert_index, slot_index], axis=1).T
-    gate_grad, up_grad, down_grad, row_dx, prob8, picks = mega(
-        tokens, out_grad, rwt, idx, gate_weight[0], up_weight[0], down_weight[0]
-    )
-    row_prob = prob8[0, :CAP]
-    pick_prob = picks.T
-    first_table, second_table = slot_table(expert_index, slot_index, expert_id, CAP)
-    select_low = (first_table + second_table).astype(jnp.bfloat16)
-    own_expert = (lax.broadcasted_iota(jnp.int32, (1, expert_count), 1) == expert_id).astype(
-        jnp.float32
-    )
-    token_dx = table_apply("cn,cd->nd", select_low, row_dx)
-    token_prob = table_apply("cn,c->n", select_low, row_prob)
-    token_term, prob_rows = in_one_piece_2(
-        (token_dx.astype(jnp.bfloat16), (token_prob[:, None] * own_expert).astype(jnp.bfloat16)),
-        "expert",
-        0,
-        1,
-    )
-    prob_rows = of_everyone(prob_rows, "tensor")
-    quarter = token_term.shape[0]
-    offset = expert_id * quarter
-    part_prob = lax.dynamic_slice_in_dim(pick_prob, offset, quarter, 0)
-    part_experts = lax.dynamic_slice_in_dim(expert_index, offset, quarter, 0)
-    part_tokens = lax.dynamic_slice_in_dim(tokens, offset, quarter, 0)
-    pick_grad = jnp.take_along_axis(prob_rows, part_experts, axis=1)
-    mixed_grad = jnp.sum(part_prob * pick_grad, axis=1, keepdims=True)
-    weights = part_prob * (pick_grad - mixed_grad)
-    onehot = (
-        part_experts[:, :, None] == lax.broadcasted_iota(jnp.int32, (1, 1, expert_count), 2)
-    ).astype(jnp.float32)
-    logit_grad = jnp.sum(onehot * weights[:, :, None], axis=1)
-    router_rows = router_weight.astype(jnp.float32)
-    tokens_grad = (token_term + jnp.dot(logit_grad, router_rows.T)).astype(jnp.bfloat16)
-    router_part = jnp.dot(part_tokens.astype(jnp.float32).T, logit_grad)
-    router_grad = of_everyone(router_part, ("dp", "expert"))
-    return (tokens_grad, router_grad, gate_grad[None], up_grad[None], down_grad[None])
+    return (tokens_grad, router_grad.T, gate_grad[None], up_grad[None], down_grad[None])
 
 
 def solution(mesh):

time: 153 us -> 108 us (0.71)
  waiting for transfers between devices: 23.7 us -> 0 us
  starting transfers between devices: 15.6 us -> 0 us
  Pallas kernels: 90.4 us -> 98.1 us
  matrix products: 5.99 us -> 0 us
  other arithmetic: 4.48 us -> 0 us
  local copies, waits for them, and re-layouts: 10.7 us -> 8.64 us
    all_to_all x3 -> x0, waiting for transfers between devices: 23.7 us -> none  [the longest x2 17.2 us: from_everyone(): lax.all_to_all(jnp.broadcast_to(array[None], (count, *array.shape)), axis...]
    all_to_all x3 -> x0, starting transfers between devices: 15.6 us -> none  [the longest x2 11.4 us: from_everyone(): lax.all_to_all(jnp.broadcast_to(array[None], (count, *array.shape)), axis...]
    pallas_call x1, Pallas kernels: 90.4 us -> 98.1 us  [shards(): pl.pallas_call(kernel, name='moe_backward', in_specs=[vm] * 5 + [hbm] * 3...]
    dot_general x6 -> x0, matrix products: 5.99 us -> none  [the longest x2 2.13 us: table_apply(): jnp.einsum(form, table_low, low_part, preferred_element_type=jnp.float32)]
    unnamed x18 -> x9, local copies, waits for them, and re-layouts: 5.89 us -> 8.64 us
  transfers between devices with their start and end apart: 3 -> 0, of which waited for: 3 -> 0; matrix products, arithmetic and copies ran while one was open for 1% -> 0% of each run, Pallas kernels for 0% -> 0%
where the time goes in v2:
time: 108 us; the launch traced here: 107 us
  Pallas kernels  98.1 us (91%)
  local copies, waits for them, and re-layouts  8.64 us (8%)
    pallas_call x1, Pallas kernels, shards(): pl.pallas_call(kernel, name='moe_backward', in_specs=[vm] * 5 + [hbm] * 3...  98.1 us
    unnamed x9, local copies, waits for them, and re-layouts  8.64 us

profile of v2, /device:TPU:1, one launch (start us, length us, event | category | flops | bytes accessed | tf_op | source)
XLA Modules:
  0.0 107.3 jit_solution(807059955523429409)
XLA Ops:
  0.6 98.1 %moe_backward.1 = (bf16[32,768]{1,0:T(8,128)(2,1)}, f32[4,768]{1,0:T(4,128)}, bf16[768,1024]{1,0:T(8,128)(2,1)}, bf16[768,1024]{1,0:T(8,128)(2,1)}, bf16[1024,768]{1,0:T(8,128)(2,1)}) custom-call(bf16[128,768]{1,0:T(8,128)(2,1)} %tok_in.1, bf16[128,768]{1,0:T(8,128)(2,1)} %og_in.1, bf16[4,768]{1,0:T(4,128)(2,1)} %bitcast.17, s32[2,128]{1,0:T(2,128)} %bitcast.18, ...), custom_call_target="tpu_custom_call" | custom-call | tf_op jit(solution)/shard_map/moe_backward/pallas_call | solution.py:547
  98.7 1.4 %copy.18 = bf16[32,768]{1,0:T(8,128)(2,1)} copy(bf16[32,768]{1,0:T(8,128)(2,1)} %get-tuple-element.20) | data formatting | bytes 98304
  100.1 1.3 %copy.19 = f32[768,4]{0,1:T(4,128)} copy(f32[768,4]{0,1:T(4,128)} %bitcast.16) | data formatting | bytes 24576
  101.4 0.0 copy-start.1
  101.4 2.8 %copy.20 = bf16[1,768,1024]{2,1,0:T(8,128)(2,1)} copy(bf16[1,768,1024]{2,1,0:T(8,128)(2,1)} %bitcast.12) | data formatting | bytes 3145728
  104.2 0.0 copy-done.1
  104.2 0.0 copy-start
  104.2 1.1 %copy.21 = bf16[1,768,1024]{2,1,0:T(8,128)(2,1)} copy(bf16[1,768,1024]{2,1,0:T(8,128)(2,1)S(1)} %bitcast.11) | data formatting | bytes 3145728
  105.4 0.8 copy-done
  106.2 1.1 %copy.22 = bf16[1,1024,768]{2,1,0:T(8,128)(2,1)} copy(bf16[1,1024,768]{2,1,0:T(8,128)(2,1)S(1)} %bitcast.10) | data formatting | bytes 3145728
Async XLA Ops:
  101.4 2.8 %copy-start.1 = (bf16[768,1024]{1,0:T(8,128)(2,1)S(1)}, bf16[768,1024]{1,0:T(8,128)(2,1)}, u32[]{:S(2)}) copy-start(bf16[768,1024]{1,0:T(8,128)(2,1)} %get-tuple-element.13) | copy-start | bytes 4718596
  104.2 2.0 %copy-start = (bf16[1024,768]{1,0:T(8,128)(2,1)S(1)}, bf16[1024,768]{1,0:T(8,128)(2,1)}, u32[]{:S(2)}) copy-start(bf16[1024,768]{1,0:T(8,128)(2,1)} %get-tuple-element.14) | copy-start | bytes 4718596

commit v3 on v2

v3 whole, which is shorter than its diff:
```python
import jax
import jax.numpy as jnp
from jax import lax
from jax.experimental import pallas as pl
from jax.experimental.pallas import tpu as pltpu
from jax.sharding import PartitionSpec as P

CAP = 96
MESH = pl.DeviceIdType.MESH
F32 = jnp.float32
BF16 = jnp.bfloat16

ORDER = (0, -1, 1, -2, 2, -3, 3, 4)
GROUPS = (1, 2, 2, 2, 1)
POS = {o: i for i, o in enumerate(ORDER)}


def place(offset):
    o = offset % 8
    return POS[o if o <= 4 else o - 8]


CHUNKS = []
_at = 0
for _n in GROUPS:
    CHUNKS.append((_at, _n))
    _at += _n

STEPS = (
    ("F", 0, 2), ("F", 0, 1), ("F", 0, 3), ("F", 0, 0), ("open",), ("D", 0, 2), ("D", 0, 1),
    ("D", 0, 3), ("D", 0, 0), ("R1", 0, 2), ("R1", 0, 1), ("R1", 0, 3), ("prob",), ("R2", 0, 0),
    ("R2", 0, 1), ("Z", 1, "t"), ("Z", 1, "g"), ("F", 1, 2), ("D", 1, 2), ("E", 0), ("F", 1, 1),
    ("D", 1, 1), ("F", 1, 3), ("D", 1, 3), ("F", 1, 0), ("D", 1, 0), ("R1", 1, 2), ("Z", 2, "t"),
    ("G", 0, 0), ("G", 0, 1), ("R1", 1, 1), ("G", 0, 2), ("G", 0, 3), ("R1", 1, 3), ("R2", 1, 0),
    ("R2", 1, 1), ("Z", 2, "g"), ("F", 2, 2), ("D", 2, 2), ("G", 0, 4), ("F", 2, 1), ("D", 2, 1),
    ("F", 2, 3), ("D", 2, 3), ("F", 2, 0), ("D", 2, 0), ("R1", 2, 2), ("X", 0), ("Z", 3, "t"),
    ("E", 1), ("R1", 2, 1), ("R1", 2, 3), ("R2", 2, 0), ("R2", 2, 1), ("Z", 3, "g"), ("F", 3, 2),
    ("D", 3, 2), ("F", 3, 1), ("D", 3, 1), ("F", 3, 3), ("D", 3, 3), ("F", 3, 0), ("D", 3, 0),
    ("G", 1, 0), ("G", 1, 1), ("R1", 3, 2), ("R1", 3, 1), ("G", 1, 2), ("G", 1, 3), ("Y", 0),
    ("R1", 3, 3), ("F", 4, 2), ("D", 4, 2), ("F", 4, 1), ("D", 4, 1), ("F", 4, 3), ("D", 4, 3),
    ("F", 4, 0), ("D", 4, 0), ("E", 2), ("R1", 4, 2), ("T",), ("R1", 4, 1), ("R1", 4, 3),
    ("G", 1, 4), ("R2", 3, 0), ("R2", 3, 1), ("X", 1), ("G", 2, 0), ("G", 2, 1), ("G", 2, 2),
    ("G", 2, 3), ("R2", 4, 0), ("R2", 4, 1), ("E", 3), ("G", 2, 4), ("E", 4), ("Y", 1), ("X", 2),
    ("G", 3, 0), ("G", 3, 1), ("G", 3, 2), ("G", 3, 3), ("G", 4, 0), ("G", 4, 1), ("P1",),
    ("G", 4, 2), ("G", 4, 3), ("G", 3, 4), ("G", 4, 4), ("P2",), ("X", 3), ("X", 4), ("P3",),
    ("Y", 2), ("W1", 0), ("W1", 1), ("W1", 2), ("P4",), ("W2", 0), ("W2", 1), ("Y", 3), ("W2", 2),
    ("W2", 3), ("P5",), ("Y", 4), ("end",),
)


def dot_nt(a, b):
    return lax.dot_general(a, b, (((1,), (1,)), ((), ())), preferred_element_type=F32)


def dot_nn(a, b):
    return lax.dot_general(a, b, (((1,), (0,)), ((), ())), preferred_element_type=F32)


class Copies:
    def __init__(self, send, recv):
        self.send, self.recv, self.count, self.made = send, recv, 0, {}

    def add(self, name, src, dst, device):
        i = self.count
        self.count += 1
        c = pltpu.make_async_remote_copy(
            src_ref=src,
            dst_ref=dst,
            send_sem=self.send.at[i],
            recv_sem=self.recv.at[i],
            device_id=device,
            device_id_type=MESH,
        )
        self.made[name] = c
        c.start()

    def got(self, name):
        self.made[name].wait_recv()

    def drain(self):
        for c in self.made.values():
            c.wait_send()


N_COPIES = 220


def kernel(
    tok_h, og_h, rwt_h, ex_h, sl_h, gw_h, uw_h, dw_h,
    tok_out, router_out, gg_o, ug_o, dg_o,
    tk, gr, sc, tkt, gw, uw, dw, part, dbuf, fa, fb, rl, rr, hh, h0t, pcol,
    lgs, lgr, prs, prr, dps, dpr, ix, yd, yr, yq, zq, own_q,
    pts, ptr, pys, pyr, ws, wr, rgs, rgr, lg3,
    tok_in, og_in, rwt, ex, sl, send_sem, recv_sem, wsem,
):
    z = lax.axis_index("dp")
    y = lax.axis_index("expert")
    t = lax.axis_index("tensor")
    x = t // 2
    c = t % 2
    right, left, across = (x + 1) % 4, (x + 3) % 4, (x + 2) % 4
    turn = (x, right, across, left)
    t_right, t_left, t_sib = right * 2 + c, left * 2 + c, x * 2 + (1 - c)

    loads = [
        pltpu.make_async_copy(a, b, wsem.at[i])
        for i, (a, b) in enumerate((
            (ex_h, ex), (sl_h, sl), (tok_h, tok_in), (og_h, og_in), (rwt_h, rwt),
            (gw_h, gw), (uw_h, uw), (dw_h, dw),
        ))
    ]
    for w in loads:
        w.start()
    wcopies = loads[5:]

    barrier = pltpu.get_barrier_semaphore()
    for k in range(1, 8):
        pl.semaphore_signal(barrier, inc=1, device_id={"dp": (z + k) % 8}, device_id_type=MESH)
        pl.semaphore_signal(barrier, inc=1, device_id={"tensor": (t + k) % 8}, device_id_type=MESH)
    for k in range(1, 4):
        pl.semaphore_signal(barrier, inc=1, device_id={"expert": (y + k) % 4}, device_id_type=MESH)

    cp = Copies(send_sem, recv_sem)

    for w in loads[:5]:
        w.wait()

    slot_at = lax.broadcasted_iota(jnp.int32, (CAP, 128), 0)
    lane_at = lax.broadcasted_iota(jnp.int32, (CAP, 128), 1)
    eye = (slot_at == lane_at).astype(F32)
    e0, e1, s0, s1 = ex[0:1, :], ex[1:2, :], sl[0:1, :], sl[1:2, :]

    def table(e, s):
        return jnp.where((e == y) & (s == slot_at), 1.0, 0.0).astype(F32)

    table0, table1 = table(e0, s0), table(e1, s1)
    select = (table0 + table1).astype(BF16)
    tk[0:CAP, :] = dot_nn(select, tok_in[...]).astype(BF16)
    gr[0:CAP, :] = dot_nn(select, og_in[...]).astype(BF16)
    lgs[4:8, :] = jnp.zeros((4, 128), F32)
    lgs[0:4, :] = dot_nt(rwt[...], tok_in[...])
    ix[0] = jnp.zeros((8, 128), jnp.int32)
    ix[0, 0:2, :] = ex[...]
    ix[0, 2:4, :] = sl[...]

    def rows_of(p):
        return pl.ds(p * CAP, CAP)

    def ring(step, which):
        buf = tk if which == "t" else gr
        cp.add(("r", step + 1, which), buf.at[rows_of(place(-step))],
               buf.at[rows_of(place(-step - 1))], {"dp": (z + 1) % 8})

    def ring_back(step, which):
        buf = tk if which == "t" else gr
        cp.add(("l", step + 1, which), buf.at[rows_of(place(step))],
               buf.at[rows_of(place(step + 1))], {"dp": (z + 7) % 8})

    def to_col(row):
        return jnp.sum(eye * row, axis=1, keepdims=True)

    def to_row(col):
        return jnp.sum(eye * col, axis=0, keepdims=True)

    def parts3(v):
        hi = v.astype(BF16)
        rest = v - hi.astype(F32)
        mid = rest.astype(BF16)
        low = (rest - mid.astype(F32)).astype(BF16)
        return hi, mid, low

    def rows8(*given):
        row = lax.broadcasted_iota(jnp.int32, (8, 128), 0)
        v = jnp.zeros((8, 128), F32)
        for i, r in enumerate(given):
            v = jnp.where(row == i, r, v)
        return v

    picks = []

    def open_up():
        pl.semaphore_wait(barrier, 17)
        for which in "tg":
            ring(0, which)
            ring_back(0, which)
        for k in range(1, 8):
            cp.add(("lg", k), lgs, lgr.at[k], {"tensor": (t + k) % 8})
        for k in range(1, 8):
            cp.add(("ix", k), ix.at[0], ix.at[place(-k)], {"dp": (z + k) % 8})

    def probabilities():
        total = lgs[0:4, :]
        for k in range(1, 8):
            cp.got(("lg", k))
            total = total + lgr[k][0:4, :]
        l0 = jnp.zeros((1, 128), F32)
        l1 = jnp.zeros((1, 128), F32)
        for j in range(4):
            l0 = l0 + jnp.where(e0 == j, total[j : j + 1, :], 0.0)
            l1 = l1 + jnp.where(e1 == j, total[j : j + 1, :], 0.0)
        p0 = jax.nn.sigmoid(l0 - l1)
        p1 = jax.nn.sigmoid(l1 - l0)
        picks.extend((p0, p1))
        low0 = p0.astype(BF16).astype(F32)
        low1 = p1.astype(BF16).astype(F32)
        col = jnp.sum(table0 * low0 + table1 * low1, axis=1, keepdims=True)
        pcol[0:CAP, :] = col
        prs[...] = jnp.broadcast_to(to_row(col), (8, 128))
        for k in range(1, 8):
            cp.add(("pr", k), prs, prr.at[place(-k)], {"dp": (z + k) % 8})

    def pass_on(d, which):
        cp.got(("r", d, which))
        if d < 3 or which == "t":
            ring(d, which)
        cp.got(("l", d, which))
        if d < 3 or which == "g":
            ring_back(d, which)

    def rows_in(k):
        p0, n = CHUNKS[k]
        return p0 * CAP, n * CAP

    def halves(k):
        r0, r = rows_in(k)
        h = r // 2
        return slice(r0, r0 + h), slice(r0 + h, r0 + r), pl.ds(r0, h), pl.ds(r0 + h, h)

    ready = []

    def forward(k, j):
        p0, n = CHUNKS[k]
        r0, r = rows_in(k)
        if not ready:
            for w in wcopies:
                w.wait()
            ready.append(1)
        if j == 2 and 4 in ORDER[p0 : p0 + n]:
            cp.got(("r", 4, "t"))
            cp.got(("l", 4, "g"))
        a = tk[r0 : r0 + r, :]
        b = gr[r0 : r0 + r, :]
        q = turn[j]
        cols = pl.ds(pl.multiple_of(q * 256, 256), 256)
        for m, v in enumerate((
            dot_nn(a, gw[:, cols]), dot_nn(a, uw[:, cols]), dot_nt(b, dw[cols, :]),
        )):
            v = v.astype(BF16)
            part[0, q, r0 : r0 + r, m * 128 : m * 128 + 128] = v[:, 0:128]
            part[1, q, r0 : r0 + r, m * 128 : m * 128 + 128] = v[:, 128:256]

    def to_sibling(k, j):
        r0, r = rows_in(k)
        rows = pl.ds(r0, r)
        q = turn[j]
        cp.add(("d", k, j), part.at[1 - c, q, rows, :], dbuf.at[q, rows, :], {"tensor": t_sib})

    def fold(target, rows, extra=None):
        v = part[c, target, rows, :].astype(F32) + dbuf[target, rows, :].astype(F32)
        if extra is not None:
            v = v + extra[rows, :].astype(F32)
        part[c, target, rows, :] = v.astype(BF16)

    def reduce_1(k, j):
        sa, sb, da, db = halves(k)
        cp.got(("d", k, j))
        if j == 2:
            fold(across, sa)
            cp.add(("fa", k), part.at[c, across, da, :], fa.at[da, :], {"tensor": t_right})
            fold(across, sb)
            cp.add(("fb", k), part.at[c, across, db, :], fb.at[db, :], {"tensor": t_left})
        if j == 1:
            fold(right, sb)
            cp.add(("rlb", k), part.at[c, right, db, :], rl.at[db, :], {"tensor": t_right})
        if j == 3:
            fold(left, sa)
            cp.add(("rra", k), part.at[c, left, da, :], rr.at[da, :], {"tensor": t_left})

    def reduce_2(k, side):
        sa, sb, da, db = halves(k)
        if side == 0:
            cp.got(("fa", k))
            fold(right, sa, fa)
            cp.add(("rla", k), part.at[c, right, da, :], rl.at[da, :], {"tensor": t_right})
        else:
            cp.got(("fb", k))
            fold(left, sb, fb)
            cp.add(("rrb", k), part.at[c, left, db, :], rr.at[db, :], {"tensor": t_left})

    def tcols(q):
        return pl.ds(pl.multiple_of(q * 128, 128), 128)

    def h_copy(name, rows, q, device):
        ref = hh.at[:, rows, tcols(q)]
        cp.add(name, ref, ref, {"tensor": device})

    def activate(k):
        p0, n = CHUNKS[k]
        sa, sb, da, db = halves(k)
        for p in range(p0, p0 + n):
            if ORDER[p] != 0:
                cp.got(("pr", (-ORDER[p]) % 8))
                pcol[p * CAP : (p + 1) * CAP, :] = to_col(prr[p][0:1, :])
        cp.got(("d", k, 0))
        sums = []
        for s, names in ((sb, ("rlb", "rrb")), (sa, ("rla", "rra"))):
            for q in names:
                cp.got((q, k))
            v = part[c, x, s, :].astype(F32) + dbuf[x, s, :].astype(F32)
            v = v + rl[s, :].astype(F32) + rr[s, :].astype(F32)
            gate, up, ga = v[:, 0:128], v[:, 128:256], v[:, 256:384]
            g = jax.nn.sigmoid(gate)
            hid = (gate * g * up).astype(BF16)
            a = pcol[s, :] * ga
            hh[0, s, tcols(t)] = hid
            hh[1, s, tcols(t)] = (a * up * g * (1.0 + gate * (1.0 - g))).astype(BF16)
            hh[2, s, tcols(t)] = (a * gate * g).astype(BF16)
            sums.insert(0, jnp.sum(hid.astype(F32) * ga, axis=1, keepdims=True))
        h_copy(("ra", k), da, t, t_right)
        h_copy(("lb", k), db, t, t_left)
        h_copy(("rb", k), db, t, t_right)
        h_copy(("la", k), da, t, t_left)
        h_copy(("so", k), pl.ds(*rows_in(k)), t, t_sib)
        col = jnp.concatenate(sums, axis=0)
        for i in range(n):
            p = p0 + i
            dps[p] = jnp.broadcast_to(to_row(col[i * CAP : (i + 1) * CAP, :]), (8, 128))
            o = ORDER[p]
            if o != 0:
                cp.add(("dp", o), dps.at[p], dpr.at[place(-o)], {"dp": (z + o) % 8})
        for p in range(p0, p0 + n):
            s = slice(p * CAP, (p + 1) * CAP)
            sc[s, :] = (pcol[s, :] * gr[s, :].astype(F32)).astype(BF16)

    def spread(k, i):
        sa, sb, da, db = halves(k)
        full = pl.ds(*rows_in(k))
        if i == 0:
            cp.got(("ra", k))
            h_copy(("xa", k), da, t_left, t_right)
        if i == 1:
            cp.got(("lb", k))
            h_copy(("xb", k), db, t_right, t_left)
        if i == 2:
            cp.got(("rb", k))
            h_copy(("sl", k), full, t_left, t_sib)
        if i == 3:
            cp.got(("la", k))
            h_copy(("sr", k), full, t_right, t_sib)
        if i == 4:
            cp.got(("xa", k))
            cp.got(("xb", k))
            h_copy(("sx", k), full, across * 2 + c, t_sib)

    def backward(k):
        p0, n = CHUNKS[k]
        r0, r = rows_in(k)
        for q in ("so", "sl", "sr", "sx"):
            cp.got((q, k))
        a = hh[1, r0 : r0 + r, :]
        b = hh[2, r0 : r0 + r, :]
        turned = []
        for p in range(p0, p0 + n):
            if ORDER[p] != 0:
                cp.got(("ix", (-ORDER[p]) % 8))
            v = ix[p]
            both = table(v[0:1, :], v[2:3, :]) + table(v[1:2, :], v[3:4, :])
            turned.append(both.T.astype(BF16))
        for m in range(3):
            cols = slice(m * 256, m * 256 + 256)
            v = (dot_nt(a, gw[cols, :]) + dot_nt(b, uw[cols, :])).astype(BF16)
            for i in range(n):
                yd[p0 + i, :, cols] = dot_nn(
                    turned[i], v[i * CAP : (i + 1) * CAP, :]).astype(BF16)
        for q in range(1, 4):
            rows = pl.ds(pl.multiple_of(((y + q) % 4) * 32, 32), 32)
            cp.add(("y", k, q), yd.at[pl.ds(p0, n), rows, :], yr.at[q, pl.ds(p0, n)],
                   {"expert": (y + q) % 4})

    def homeward(k):
        p0, n = CHUNKS[k]
        for q in range(1, 4):
            cp.got(("y", k, q))
        rows = pl.ds(pl.multiple_of(y * 32, 32), 32)
        for p in range(p0, p0 + n):
            v = yd[p, rows, :].astype(F32)
            for q in range(1, 4):
                v = v + yr[q, p].astype(F32)
            o = ORDER[p]
            if o == 0:
                own_q[...] = v
            else:
                yq[p] = v.astype(BF16)
                cp.add(("z", o), yq.at[p], zq.at[place(-o)], {"dp": (z + o) % 8})

    def router_1():
        total = dps[0][0:1, :]
        for p in range(8):
            if ORDER[p] != 0:
                o = ORDER[p]
                cp.got(("dp", -o if o != 4 else 4))
                total = total + dpr[p][0:1, :]
        col = to_col(total)
        pts[...] = rows8(jnp.sum(table0 * col, axis=0, keepdims=True),
                         jnp.sum(table1 * col, axis=0, keepdims=True))
        for k in range(1, 8):
            cp.add(("pt", k), pts, ptr.at[k], {"tensor": (t + k) % 8})

    def router_2():
        total = pts[...]
        for k in range(1, 8):
            cp.got(("pt", k))
            total = total + ptr[k]
        pys[...] = total
        for k in range(1, 4):
            cp.add(("py", k), pys, pyr.at[k], {"expert": (y + k) % 4})

    def router_3():
        total = pys[...]
        for k in range(1, 4):
            cp.got(("py", k))
            total = total + pyr[k]
        d0, d1 = total[0:1, :], total[1:2, :]
        p0, p1 = picks
        mixed = p0 * d0 + p1 * d1
        w0 = p0 * (d0 - mixed)
        w1 = p1 * (d1 - mixed)
        ws[...] = jnp.broadcast_to(
            to_row(jnp.sum(table0 * w0 + table1 * w1, axis=1, keepdims=True)), (8, 128))
        for k in range(1, 8):
            cp.add(("w", k), ws, wr.at[place(-k)], {"dp": (z + k) % 8})
        i0 = lax.broadcasted_iota(jnp.int32, (128, 128), 0)
        i1 = lax.broadcasted_iota(jnp.int32, (128, 128), 1)
        eye_t = (i0 == i1).astype(F32)

        def col_t(row):
            return jnp.sum(eye_t * row, axis=1, keepdims=True)

        lane = lax.broadcasted_iota(jnp.int32, (128, 16), 1)
        of_expert = (lane % 4).astype(F32)
        v = (jnp.where(col_t(e0.astype(F32)) == of_expert, col_t(w0), 0.0)
             + jnp.where(col_t(e1.astype(F32)) == of_expert, col_t(w1), 0.0))
        hi, mid, low = (q.astype(F32) for q in parts3(v))
        lg3[...] = jnp.where(lane < 4, hi, jnp.where(lane < 8, mid, jnp.where(lane < 12, low, 0.0)))

    def router_4():
        acc = jnp.zeros((8, 768), F32)
        for p in range(8):
            if ORDER[p] == 0:
                v = ws[0:1, :]
            else:
                cp.got(("w", (-ORDER[p]) % 8))
                v = wr[p][0:1, :]
            lhs = rows8(*(q.astype(F32) for q in parts3(v)))
            acc = acc + dot_nn(lhs[:, 0:CAP].astype(BF16), tk[p * CAP : (p + 1) * CAP, :])
        rgs[...] = jnp.broadcast_to(jnp.sum(acc, axis=0, keepdims=True), (8, 768))
        rgr[0] = rgs[...]
        for k in range(1, 4):
            cp.add(("rg", k), rgs, rgr.at[k], {"expert": (y + k) % 4})

    def router_5():
        for k in range(1, 4):
            cp.got(("rg", k))
        for j in range(4):
            k = (y + 4 - j) % 4
            router_out[j : j + 1, :] = rgr[k][0:1, :]

    def finish():
        rows = pl.ds(pl.multiple_of(y * 32, 32), 32)
        total = own_q[...]
        total = total + dot_nn(lg3[rows, :].astype(BF16), jnp.concatenate([rwt[...]] * 4, axis=0))
        for p in range(8):
            o = ORDER[p]
            if o != 0:
                cp.got(("z", -o if o != 4 else 4))
                total = total + zq[p].astype(F32)
        tok_out[...] = total.astype(BF16)

    def turn_tokens():
        @pl.loop(0, 3)
        def _(n):
            cols = pl.ds(pl.multiple_of(n * 256, 256), 256)
            tkt[cols, :] = tk[:, cols].T

    def weights_1(i):
        rows = slice(i * 256, i * 256 + 256)
        lhs = tkt[rows, :]

        @pl.loop(0, 4)
        def _(n):
            cols = pl.ds(pl.multiple_of(n * 256, 256), 256)
            gg_o[rows, cols] = dot_nn(lhs, hh[1, :, cols]).astype(BF16)
            ug_o[rows, cols] = dot_nn(lhs, hh[2, :, cols]).astype(BF16)

    def weights_2(i):
        rows = slice(i * 256, i * 256 + 256)
        h0t[...] = hh[0, :, rows].T

        @pl.loop(0, 3)
        def _(n):
            cols = pl.ds(pl.multiple_of(n * 256, 256), 256)
            dg_o[rows, cols] = dot_nn(h0t[...], sc[:, cols]).astype(BF16)

    run = {
        "open": open_up, "prob": probabilities, "Z": pass_on, "F": forward, "D": to_sibling,
        "R1": reduce_1, "R2": reduce_2, "E": activate, "G": spread, "X": backward,
        "Y": homeward, "P1": router_1, "P2": router_2, "P3": router_3, "P4": router_4,
        "P5": router_5, "T": turn_tokens, "W1": weights_1, "W2": weights_2, "end": finish,
    }
    for step in STEPS:
        run[step[0]](*step[1:])
    cp.drain()


def put_out(*refs):
    sem = refs[10]
    copies = [pltpu.make_async_copy(refs[i], refs[5 + i], sem.at[i]) for i in range(5)]
    for q in copies:
        q.start()
    for q in copies:
        q.wait()


def shards(
    tokens, out_grad, router_weight, gate_weight, up_weight, down_weight, expert_index, slot_index
):
    vm = pl.BlockSpec(memory_space=pltpu.VMEM)
    hbm = pl.BlockSpec(memory_space=pltpu.HBM)
    V = pltpu.VMEM
    small = V((8, 128), F32)
    several = V((8, 8, 128), F32)
    out_shape = [
        jax.ShapeDtypeStruct((32, 768), BF16),
        jax.ShapeDtypeStruct((4, 768), F32),
        jax.ShapeDtypeStruct((768, 1024), BF16),
        jax.ShapeDtypeStruct((768, 1024), BF16),
        jax.ShapeDtypeStruct((1024, 768), BF16),
    ]
    results = pl.pallas_call(
        kernel,
        name="moe_backward",
        in_specs=[hbm] * 8,
        out_specs=[vm] * 5,
        out_shape=out_shape,
        scratch_shapes=[
            V((768, 768), BF16), V((768, 768), BF16), V((768, 768), BF16), V((768, 768), BF16),
            V((768, 1024), BF16), V((768, 1024), BF16), V((1024, 768), BF16),
            V((2, 4, 768, 384), BF16), V((4, 768, 384), BF16),
            V((768, 384), BF16), V((768, 384), BF16), V((768, 384), BF16), V((768, 384), BF16),
            V((3, 768, 1024), BF16), V((256, 768), BF16), V((768, 1), F32),
            small, several, small, several, several, several, V((8, 8, 128), jnp.int32),
            V((8, 128, 768), BF16), V((4, 8, 32, 768), BF16), V((8, 32, 768), BF16),
            V((8, 32, 768), BF16), V((32, 768), F32),
            small, several, small, V((4, 8, 128), F32), small, several,
            V((8, 768), F32), V((4, 8, 768), F32), V((128, 16), F32),
            V((128, 768), BF16), V((128, 768), BF16), V((4, 768), BF16),
            V((2, 128), jnp.int32), V((2, 128), jnp.int32),
            pltpu.SemaphoreType.DMA((N_COPIES,)), pltpu.SemaphoreType.DMA((N_COPIES,)),
            pltpu.SemaphoreType.DMA((8,)),
        ],
        compiler_params=pltpu.CompilerParams(
            collective_id=0, has_side_effects=True, vmem_limit_bytes=40 * 1024 * 1024
        ),
    )(
        *(pltpu.with_memory_space_constraint(v, pltpu.HBM) for v in (
            tokens, out_grad, router_weight.T, expert_index.T, slot_index.T,
            gate_weight[0], up_weight[0], down_weight[0],
        ))
    )
    tokens_grad, router_grad, gate_grad, up_grad, down_grad = pl.pallas_call(
        put_out,
        name="put_out",
        in_specs=[vm] * 5,
        out_specs=[hbm] * 5,
        out_shape=out_shape,
        scratch_shapes=[pltpu.SemaphoreType.DMA((5,))],
        compiler_params=pltpu.CompilerParams(vmem_limit_bytes=1024 * 1024),
    )(*results)
    return (tokens_grad, router_grad.T, gate_grad[None], up_grad[None], down_grad[None])


def solution(mesh):
    in_specs = (
        P("dp", "tensor"),
        P("dp", "tensor"),
        P("tensor", None),
        P("expert", "tensor", "dp"),
        P("expert", "tensor", "dp"),
        P("expert", "dp", "tensor"),
        P("dp", None),
        P("dp", None),
    )
    out_specs = (
        P(("dp", "expert"), "tensor"),
        P("tensor", None),
        P("expert", "tensor", "dp"),
        P("expert", "tensor", "dp"),
        P("expert", "dp", "tensor"),
    )
    return jax.shard_map(shards, mesh=mesh, in_specs=in_specs, out_specs=out_specs, check_vma=False)
```

time: 108 us -> 92.8 us (0.86)
  local copies, waits for them, and re-layouts: 8.64 us -> 0 us
  Pallas kernels: 98.1 us -> 92 us
    unnamed x9 -> x0, local copies, waits for them, and re-layouts: 8.64 us -> none
    pallas_call x1 -> x2, Pallas kernels: 98.1 us -> 92 us  [the longest x1 89.7 us: shards(): pl.pallas_call(kernel, name='moe_backward', in_specs=[hbm] * 8, out_specs...]
where the time goes in v3:
time: 92.8 us
  Pallas kernels  92 us (99%)
    pallas_call x1, Pallas kernels, shards(): pl.pallas_call(kernel, name='moe_backward', in_specs=[hbm] * 8, out_specs...  89.7 us
    pallas_call x1, Pallas kernels, shards(): pl.pallas_call(put_out, name='put_out', in_specs=[vm] * 5, out_specs=[hbm...  2.25 us

profile of v3, /device:TPU:1, one launch (start us, length us, event | category | flops | bytes accessed | tf_op | source)
XLA Modules:
  0.0 92.8 jit_solution(4525405596946171806)
XLA Ops:
  0.6 89.7 %moe_backward.1 = (bf16[32,768]{1,0:T(8,128)(2,1)S(1)}, f32[4,768]{1,0:T(4,128)S(1)}, bf16[768,1024]{1,0:T(8,128)(2,1)S(1)}, bf16[768,1024]{1,0:T(8,128)(2,1)S(1)}, bf16[1024,768]{1,0:T(8,128)(2,1)S(1)}) custom-call(bf16[128,768]{1,0:T(8,128)(2,1)} %tok_h.1, bf16[128,768]{1,0:T(8,128)(2,1)} %og_h.1, bf16[4,768]{1,0:T(4,128)(2,1)} %bitcast.13, ...), custom_call_target="tpu_custom_call" | custom-call | tf_op jit(solution)/shard_map/moe_backward/pallas_call | solution.py:539
  90.4 2.2 %put_out.1 = (bf16[32,768]{1,0:T(8,128)(2,1)}, f32[4,768]{1,0:T(4,128)}, bf16[768,1024]{1,0:T(8,128)(2,1)}, bf16[768,1024]{1,0:T(8,128)(2,1)}, bf16[1024,768]{1,0:T(8,128)(2,1)}) custom-call(bf16[32,768]{1,0:T(8,128)(2,1)S(1)} %get-tuple-element.15.refs_0_, f32[4,768]{1,0:T(4,128)S(1)} %get-tuple-element.16.refs_1_, ...), custom_call_target="tpu_custom_call" | custom-call | tf_op jit(solution)/shard_map/put_out/pallas_call | solution.py:570

commit v4 on v3

v4 whole, which is shorter than its diff:
```python
import jax
import jax.numpy as jnp
from jax import lax
from jax.experimental import pallas as pl
from jax.experimental.pallas import tpu as pltpu
from jax.sharding import PartitionSpec as P

CAP = 96
MESH = pl.DeviceIdType.MESH
F32 = jnp.float32
BF16 = jnp.bfloat16

UNITS = ((0, 0), (0, 1), (-1, 0), (1, 0), (-1, 1), (1, 1), (-2, 0), (2, 0), (-2, 1), (2, 1), (4, 0), (4, 1), (-3, 0), (-3, 1), (3, 0), (3, 1))
GROUPS = (2, 2, 2, 2, 2, 2, 2, 2)
BACK = (1, 2, 2, 1, 1, 1)
HALF = CAP // 2
BLOCKS = (0, -1, 1, -2, 2, -3, 3, 4)
POS = {o: i for i, o in enumerate(BLOCKS)}
ROW = {u: i * HALF for i, u in enumerate(UNITS)}


def near(offset):
    o = offset % 8
    return o if o <= 4 else o - 8


def place(offset):
    return POS[near(offset)]


def runs(sizes):
    ends = [sum(sizes[: i + 1]) for i in range(len(sizes))]
    return [(e - n, n) for e, n in zip(ends, sizes)]


CHUNKS = runs(GROUPS)
BACKS = runs(BACK)

STEPS = (
    ("open",), ("F", 0, 2), ("D", 0, 2), ("F", 0, 1), ("D", 0, 1), ("F", 0, 3), ("D", 0, 3),
    ("F", 0, 0), ("D", 0, 0), ("S", 0), ("R1", 0, 2), ("R1", 0, 1), ("R1", 0, 3), ("R2", 0, 0),
    ("R2", 0, 1), ("Z", 1, 0), ("prob",), ("far", 2), ("F", 1, 2), ("D", 1, 2), ("F", 1, 1),
    ("D", 1, 1), ("F", 1, 3), ("D", 1, 3), ("F", 1, 0), ("D", 1, 0), ("R1", 1, 2), ("R1", 1, 1),
    ("E", 0), ("R1", 1, 3), ("Z", 1, 1), ("F", 2, 2), ("D", 2, 2), ("F", 2, 1), ("D", 2, 1),
    ("F", 2, 3), ("D", 2, 3), ("F", 2, 0), ("D", 2, 0), ("S", 1), ("S", 2), ("R1", 2, 2),
    ("R2", 1, 0), ("R2", 1, 1), ("R1", 2, 1), ("R1", 2, 3), ("G", 0, 1), ("Z", 2, 0), ("far", 3),
    ("F", 3, 2), ("D", 3, 2), ("G", 0, 0), ("G", 0, 3), ("F", 3, 1), ("D", 3, 1), ("F", 3, 3),
    ("D", 3, 3), ("G", 0, 2), ("F", 3, 0), ("D", 3, 0), ("R1", 3, 2), ("R2", 2, 0), ("R2", 2, 1),
    ("R1", 3, 1), ("E", 1), ("Z", 2, 1), ("R1", 3, 3), ("F", 4, 2), ("D", 4, 2), ("F", 4, 1),
    ("D", 4, 1), ("F", 4, 3), ("D", 4, 3), ("G", 0, 4), ("F", 4, 0), ("D", 4, 0), ("S", 3),
    ("S", 4), ("R1", 4, 2), ("R2", 3, 0), ("R2", 3, 1), ("R1", 4, 1), ("R1", 4, 3), ("E", 2),
    ("Z", 3, 0), ("far", 4), ("G", 1, 1), ("X", 0), ("G", 1, 0), ("G", 1, 3), ("G", 1, 2),
    ("R2", 4, 0), ("R2", 4, 1), ("Z", 3, 1), ("E", 3), ("G", 2, 0), ("G", 2, 1), ("V", 0),
    ("G", 2, 2), ("G", 2, 3), ("G", 1, 4), ("E", 4), ("G", 3, 0), ("G", 3, 1), ("F", 5, 2),
    ("D", 5, 2), ("Y", 0), ("G", 3, 2), ("G", 3, 3), ("F", 5, 1), ("D", 5, 1), ("F", 5, 3),
    ("D", 5, 3), ("G", 2, 4), ("F", 5, 0), ("D", 5, 0), ("R1", 5, 2), ("F", 6, 2), ("D", 6, 2),
    ("F", 6, 1), ("D", 6, 1), ("G", 4, 0), ("G", 4, 1), ("F", 6, 3), ("D", 6, 3), ("R1", 5, 1),
    ("F", 6, 0), ("D", 6, 0), ("G", 4, 2), ("G", 4, 3), ("R1", 5, 3), ("F", 7, 2), ("D", 7, 2),
    ("G", 3, 4), ("R1", 6, 2), ("R1", 6, 1), ("R2", 5, 0), ("R2", 5, 1), ("R1", 6, 3), ("X", 1),
    ("G", 4, 4), ("R1", 7, 2), ("F", 7, 1), ("D", 7, 1), ("F", 7, 3), ("D", 7, 3), ("R2", 6, 0),
    ("R2", 6, 1), ("F", 7, 0), ("D", 7, 0), ("S", 5), ("R1", 7, 1), ("R1", 7, 3), ("E", 5),
    ("R2", 7, 0), ("R2", 7, 1), ("X", 2), ("E", 6), ("V", 1), ("S", 6), ("S", 7), ("G", 5, 0),
    ("G", 5, 1), ("G", 5, 2), ("G", 5, 3), ("E", 7), ("G", 6, 0), ("G", 6, 1), ("V", 2),
    ("G", 6, 2), ("G", 6, 3), ("G", 5, 4), ("Y", 1), ("G", 7, 0), ("G", 7, 1), ("X", 3),
    ("G", 7, 2), ("G", 6, 4), ("G", 7, 3), ("Y", 2), ("P1",), ("G", 7, 4), ("X", 4), ("V", 3),
    ("X", 5), ("W", 0, 0), ("P3",), ("W", 0, 1), ("V", 4), ("W", 0, 2), ("W", 1, 0), ("Y", 3),
    ("W", 1, 1), ("V", 5), ("W", 1, 2), ("W", 2, 0), ("W", 2, 1), ("Y", 4), ("W", 2, 2),
    ("W", 2, 3), ("Y", 5), ("P5",), ("end",),
)


def dot_nt(a, b):
    return lax.dot_general(a, b, (((1,), (1,)), ((), ())), preferred_element_type=F32)


def dot_nn(a, b):
    return lax.dot_general(a, b, (((1,), (0,)), ((), ())), preferred_element_type=F32)


class Copies:
    def __init__(self, send, recv):
        self.send, self.recv, self.count, self.made = send, recv, 0, {}

    def add(self, name, src, dst, device):
        i = self.count
        self.count += 1
        c = pltpu.make_async_remote_copy(
            src_ref=src,
            dst_ref=dst,
            send_sem=self.send.at[i],
            recv_sem=self.recv.at[i],
            device_id=device,
            device_id_type=MESH,
        )
        self.made[name] = c
        c.start()

    def got(self, name):
        self.made[name].wait_recv()

    def drain(self):
        for c in self.made.values():
            c.wait_send()


N_COPIES = 340


def kernel(
    tok_h, og_h, rwt_h, ex_h, sl_h, gw_h, uw_h, dw_h,
    tok_out, router_out, gg_o, ug_o, dg_o,
    tk, gr, sc, gw, uw, dw, part, dbuf, fa, fb, rl, rr, hh, pcol, dcol,
    lgs, lgr, prs, prr, dps, dpr, ix, selt, dxs, yq, zq, own_q,
    pts, ptr, rgs, rgr, lg3,
    tok_in, og_in, rwt, ex, sl, send_sem, recv_sem, wsem, *sums,
):
    yd, ya, yb, yr, yl = (sums[i * len(BACKS) : (i + 1) * len(BACKS)] for i in range(5))
    z = lax.axis_index("dp")
    y = lax.axis_index("expert")
    t = lax.axis_index("tensor")
    x = t // 2
    c = t % 2
    right, left, across = (x + 1) % 4, (x + 3) % 4, (x + 2) % 4
    turn = (x, right, across, left)
    t_right, t_left, t_sib = right * 2 + c, left * 2 + c, x * 2 + (1 - c)

    loads = [
        pltpu.make_async_copy(a, b, wsem.at[i])
        for i, (a, b) in enumerate((
            (ex_h, ex), (sl_h, sl), (tok_h, tok_in), (og_h, og_in), (rwt_h, rwt),
            (gw_h, gw), (uw_h, uw), (dw_h, dw),
        ))
    ]
    for w in loads:
        w.start()
    wcopies = loads[5:]

    barrier = pltpu.get_barrier_semaphore()
    for k in (1, 7):
        pl.semaphore_signal(barrier, inc=1, device_id={"dp": (z + k) % 8}, device_id_type=MESH)
    for k in range(1, 32):
        pl.semaphore_signal(
            barrier, inc=1, device_id={"expert": (y + k // 8) % 4, "tensor": (t + k) % 8},
            device_id_type=MESH)

    cp = Copies(send_sem, recv_sem)

    for w in loads[:5]:
        w.wait()

    slot_at = lax.broadcasted_iota(jnp.int32, (CAP, 128), 0)
    lane_at = lax.broadcasted_iota(jnp.int32, (CAP, 128), 1)
    eye = (slot_at == lane_at).astype(F32)
    e0, e1, s0, s1 = ex[0:1, :], ex[1:2, :], sl[0:1, :], sl[1:2, :]

    def table(e, s):
        return jnp.where((e == y) & (s == slot_at), 1.0, 0.0).astype(F32)

    table0, table1 = table(e0, s0), table(e1, s1)
    select = (table0 + table1).astype(BF16)
    tk[0:CAP, :] = dot_nn(select, tok_in[...]).astype(BF16)
    gr[0:CAP, :] = dot_nn(select, og_in[...]).astype(BF16)
    lgs[4:8, :] = jnp.zeros((4, 128), F32)
    lgs[0:4, :] = dot_nt(rwt[...], tok_in[...])
    ix[0] = jnp.zeros((8, 128), jnp.int32)
    ix[0, 0:2, :] = ex[...]
    ix[0, 2:4, :] = sl[...]

    def ring(step, half):
        for which, buf in (("t", tk), ("g", gr)):
            cp.add(("r", step + 1, half, which), buf.at[pl.ds(ROW[near(-step), half], HALF)],
                   buf.at[pl.ds(ROW[near(-step - 1), half], HALF)], {"dp": (z + 1) % 8})

    def ring_back(step, half):
        for which, buf in (("t", tk), ("g", gr)):
            cp.add(("l", step + 1, half, which), buf.at[pl.ds(ROW[near(step), half], HALF)],
                   buf.at[pl.ds(ROW[near(step + 1), half], HALF)], {"dp": (z + 7) % 8})

    def to_col(row):
        return jnp.sum(eye * row, axis=1, keepdims=True)

    def to_row(col):
        return jnp.sum(eye * col, axis=0, keepdims=True)

    def parts3(v):
        hi = v.astype(BF16)
        rest = v - hi.astype(F32)
        mid = rest.astype(BF16)
        low = (rest - mid.astype(F32)).astype(BF16)
        return hi, mid, low

    def rows8(*given):
        row = lax.broadcasted_iota(jnp.int32, (8, 128), 0)
        v = jnp.zeros((8, 128), F32)
        for i, r in enumerate(given):
            v = jnp.where(row == i, r, v)
        return v

    picks = []

    def open_up():
        pl.semaphore_wait(barrier, 33)
        for k in (1, 7):
            cp.add(("ix", k), ix.at[0], ix.at[place(-k)], {"dp": (z + k) % 8})
        for half in range(2):
            ring(0, half)
            ring_back(0, half)
        for k in range(1, 8):
            cp.add(("lg", k), lgs, lgr.at[k], {"tensor": (t + k) % 8})

    def probabilities():
        total = lgs[0:4, :]
        for k in range(1, 8):
            cp.got(("lg", k))
            total = total + lgr[k][0:4, :]
        l0 = jnp.zeros((1, 128), F32)
        l1 = jnp.zeros((1, 128), F32)
        for j in range(4):
            l0 = l0 + jnp.where(e0 == j, total[j : j + 1, :], 0.0)
            l1 = l1 + jnp.where(e1 == j, total[j : j + 1, :], 0.0)
        p0 = jax.nn.sigmoid(l0 - l1)
        p1 = jax.nn.sigmoid(l1 - l0)
        picks.extend((p0, p1))
        low0 = p0.astype(BF16).astype(F32)
        low1 = p1.astype(BF16).astype(F32)
        col = jnp.sum(table0 * low0 + table1 * low1, axis=1, keepdims=True)
        pcol[0:CAP, :] = col
        prs[...] = jnp.broadcast_to(to_row(col), (8, 128))
        for k in (1, 7):
            cp.add(("pr", k), prs, prr.at[place(-k)], {"dp": (z + k) % 8})

    def far(d):
        for k in sorted({d, 8 - d}):
            cp.add(("ix", k), ix.at[0], ix.at[place(-k)], {"dp": (z + k) % 8})
            cp.add(("pr", k), prs, prr.at[place(-k)], {"dp": (z + k) % 8})

    def pass_on(d, half):
        for which in "tg":
            cp.got(("r", d, half, which))
        if d < 3 or half == 0:
            ring(d, half)
        for which in "tg":
            cp.got(("l", d, half, which))
        if d < 3 or half == 1:
            ring_back(d, half)

    def rows_in(k):
        u0, n = CHUNKS[k]
        return u0 * HALF, n * HALF

    def units_in(k):
        u0, n = CHUNKS[k]
        return UNITS[u0 : u0 + n]

    def halves(k):
        r0, r = rows_in(k)
        h = r // 2
        return slice(r0, r0 + h), slice(r0 + h, r0 + r), pl.ds(r0, h), pl.ds(r0 + h, h)

    blocks_seen, halves_seen = set(), set()

    ready = []

    def forward(k, j):
        r0, r = rows_in(k)
        if not ready:
            for w in wcopies:
                w.wait()
            ready.append(1)
        for o, half in units_in(k):
            if j == 2 and o == 4:
                for which in "tg":
                    cp.got(("rl"[half], 4, half, which))
        a = tk[r0 : r0 + r, :]
        b = gr[r0 : r0 + r, :]
        q = turn[j]
        cols = pl.ds(pl.multiple_of(q * 256, 256), 256)
        for m, v in enumerate((
            dot_nn(a, gw[:, cols]), dot_nn(a, uw[:, cols]), dot_nt(b, dw[cols, :]),
        )):
            v = v.astype(BF16)
            part[0, q, r0 : r0 + r, m * 128 : m * 128 + 128] = v[:, 0:128]
            part[1, q, r0 : r0 + r, m * 128 : m * 128 + 128] = v[:, 128:256]

    def to_sibling(k, j):
        r0, r = rows_in(k)
        rows = pl.ds(r0, r)
        q = turn[j]
        cp.add(("d", k, j), part.at[1 - c, q, rows, :], dbuf.at[q, rows, :], {"tensor": t_sib})

    def fold(target, rows, extra=None):
        v = part[c, target, rows, :].astype(F32) + dbuf[target, rows, :].astype(F32)
        if extra is not None:
            v = v + extra[rows, :].astype(F32)
        part[c, target, rows, :] = v.astype(BF16)

    def reduce_1(k, j):
        sa, sb, da, db = halves(k)
        cp.got(("d", k, j))
        if j == 2:
            fold(across, sa)
            cp.add(("fa", k), part.at[c, across, da, :], fa.at[da, :], {"tensor": t_right})
            fold(across, sb)
            cp.add(("fb", k), part.at[c, across, db, :], fb.at[db, :], {"tensor": t_left})
        if j == 1:
            fold(right, sb)
            cp.add(("rlb", k), part.at[c, right, db, :], rl.at[db, :], {"tensor": t_right})
        if j == 3:
            fold(left, sa)
            cp.add(("rra", k), part.at[c, left, da, :], rr.at[da, :], {"tensor": t_left})

    def reduce_2(k, side):
        sa, sb, da, db = halves(k)
        if side == 0:
            cp.got(("fa", k))
            fold(right, sa, fa)
            cp.add(("rla", k), part.at[c, right, da, :], rl.at[da, :], {"tensor": t_right})
        else:
            cp.got(("fb", k))
            fold(left, sb, fb)
            cp.add(("rrb", k), part.at[c, left, db, :], rr.at[db, :], {"tensor": t_left})

    def tcols(q):
        return pl.ds(pl.multiple_of(q * 128, 128), 128)

    def h_copy(name, rows, q, device):
        ref = hh.at[:, rows, tcols(q)]
        cp.add(name, ref, ref, {"tensor": device})

    def activate(k):
        sa, sb, da, db = halves(k)
        for o, half in units_in(k):
            if o != 0 and o not in blocks_seen:
                blocks_seen.add(o)
                cp.got(("pr", (-o) % 8))
                col = to_col(prr[POS[o]][0:1, :])
                for i in range(2):
                    pcol[ROW[o, i] : ROW[o, i] + HALF, :] = col[i * HALF : (i + 1) * HALF, :]
        cp.got(("d", k, 0))
        sums = []
        for s, names in ((sb, ("rlb", "rrb")), (sa, ("rla", "rra"))):
            for q in names:
                cp.got((q, k))
            v = part[c, x, s, :].astype(F32) + dbuf[x, s, :].astype(F32)
            v = v + rl[s, :].astype(F32) + rr[s, :].astype(F32)
            gate, up, ga = v[:, 0:128], v[:, 128:256], v[:, 256:384]
            g = jax.nn.sigmoid(gate)
            hid = (gate * g * up).astype(BF16)
            a = pcol[s, :] * ga
            hh[0, s, tcols(t)] = hid
            hh[1, s, tcols(t)] = (a * up * g * (1.0 + gate * (1.0 - g))).astype(BF16)
            hh[2, s, tcols(t)] = (a * gate * g).astype(BF16)
            sums.insert(0, jnp.sum(hid.astype(F32) * ga, axis=1, keepdims=True))
        h_copy(("ra", k), da, t, t_right)
        h_copy(("lb", k), db, t, t_left)
        h_copy(("rb", k), db, t, t_right)
        h_copy(("la", k), da, t, t_left)
        h_copy(("so", k), pl.ds(*rows_in(k)), t, t_sib)
        dcol[sa, :] = sums[0]
        dcol[sb, :] = sums[1]
        for o, half in units_in(k):
            halves_seen.add((o, half))
            if (o, 1 - half) in halves_seen:
                col = jnp.concatenate(
                    [dcol[ROW[o, i] : ROW[o, i] + HALF, :] for i in range(2)], axis=0)
                p = POS[o]
                dps[p] = jnp.broadcast_to(to_row(col), (8, 128))
                if o != 0:
                    cp.add(("dp", o), dps.at[p], dpr.at[place(-o)], {"dp": (z + o) % 8})
        r0, r = rows_in(k)
        s = slice(r0, r0 + r)
        sc[s, :] = (pcol[s, :] * gr[s, :].astype(F32)).astype(BF16)

    def spread(k, i):
        sa, sb, da, db = halves(k)
        full = pl.ds(*rows_in(k))
        if i == 0:
            cp.got(("ra", k))
            h_copy(("xa", k), da, t_left, t_right)
        if i == 1:
            cp.got(("lb", k))
            h_copy(("xb", k), db, t_right, t_left)
        if i == 2:
            cp.got(("rb", k))
            h_copy(("sl", k), full, t_left, t_sib)
        if i == 3:
            cp.got(("la", k))
            h_copy(("sr", k), full, t_right, t_sib)
        if i == 4:
            cp.got(("xa", k))
            cp.got(("xb", k))
            h_copy(("sx", k), full, across * 2 + c, t_sib)

    def tables(p):
        o = BLOCKS[p]
        if o != 0:
            cp.got(("ix", (-o) % 8))
        v = ix[p]
        both = table(v[0:1, :], v[2:3, :]) + table(v[1:2, :], v[3:4, :])
        selt[p] = both.T.astype(BF16)

    def chunks_in(m):
        k0, n = BACKS[m]
        return range(k0, k0 + n)

    def blocks_in(m):
        return [o for k in chunks_in(m) for o, half in units_in(k) if half == 0]

    def backward(m):
        for k in chunks_in(m):
            for q in ("so", "sl", "sr", "sx"):
                cp.got((q, k))
        r0 = rows_in(chunks_in(m)[0])[0]
        r = sum(rows_in(k)[1] for k in chunks_in(m))
        a = hh[1, r0 : r0 + r, :]
        b = hh[2, r0 : r0 + r, :]
        for i in range(3):
            cols = slice(i * 256, i * 256 + 256)
            dxs[r0 : r0 + r, cols] = (dot_nt(a, gw[cols, :]) + dot_nt(b, uw[cols, :])).astype(BF16)
        for i, o in enumerate(blocks_in(m)):
            v = jnp.concatenate([dxs[ROW[o, h] : ROW[o, h] + HALF, :] for h in range(2)], axis=0)
            yd[m][i] = dot_nn(selt[POS[o]], v).astype(BF16)

        def piece(q, low):
            return yd[m].at[:, pl.ds(pl.multiple_of(((y + q) % 4) * 32 + low, 16), 16), :]

        cp.add(("ya", m), piece(2, 0), ya[m], {"expert": (y + 1) % 4})
        cp.add(("yb", m), piece(2, 16), yb[m], {"expert": (y + 3) % 4})
        cp.add(("yr", m), piece(1, 16), yr[m].at[:, pl.ds(16, 16), :], {"expert": (y + 1) % 4})
        cp.add(("yl", m), piece(3, 0), yl[m].at[:, pl.ds(0, 16), :], {"expert": (y + 3) % 4})

    def relay(m):
        for name, q, low, buf, put in (("ya", 1, 0, ya, yr), ("yb", 3, 16, yb, yl)):
            cp.got((name, m))
            rows = pl.ds(pl.multiple_of(((y + q) % 4) * 32 + low, 16), 16)
            for i in range(len(blocks_in(m))):
                yd[m][i, rows, :] = (
                    yd[m][i, rows, :].astype(F32) + buf[m][i].astype(F32)).astype(BF16)
            cp.add((name, m, 2), yd[m].at[:, rows, :], put[m].at[:, pl.ds(low, 16), :],
                   {"expert": (y + q) % 4})

    def homeward(m):
        for name in (("yr", m), ("yl", m), ("ya", m, 2), ("yb", m, 2)):
            cp.got(name)
        rows = pl.ds(pl.multiple_of(y * 32, 32), 32)
        for i, o in enumerate(blocks_in(m)):
            v = yd[m][i, rows, :].astype(F32) + yr[m][i].astype(F32) + yl[m][i].astype(F32)
            if o == 0:
                own_q[...] = v
            else:
                yq[POS[o]] = v.astype(BF16)
                cp.add(("z", o), yq.at[POS[o]], zq.at[place(-o)], {"dp": (z + o) % 8})

    def router_1():
        total = dps[0][0:1, :]
        for p in range(8):
            if BLOCKS[p] != 0:
                o = BLOCKS[p]
                cp.got(("dp", -o if o != 4 else 4))
                total = total + dpr[p][0:1, :]
        col = to_col(total)
        pts[...] = rows8(jnp.sum(table0 * col, axis=0, keepdims=True),
                         jnp.sum(table1 * col, axis=0, keepdims=True))
        for k in range(1, 32):
            cp.add(("pt", k), pts, ptr.at[k],
                   {"expert": (y + k // 8) % 4, "tensor": (t + k) % 8})

    def router_3():
        total = pts[...]
        for k in range(1, 32):
            cp.got(("pt", k))
        for k in range(1, 32):
            total = total + ptr[k]
        d0, d1 = total[0:1, :], total[1:2, :]
        p0, p1 = picks
        mixed = p0 * d0 + p1 * d1
        w0 = p0 * (d0 - mixed)
        w1 = p1 * (d1 - mixed)
        grads = [jnp.where(e0 == j, w0, 0.0) + jnp.where(e1 == j, w1, 0.0) for j in range(4)]
        split = [parts3(v) for v in grads]
        row = lax.broadcasted_iota(jnp.int32, (16, 128), 0)
        lhs = jnp.zeros((16, 128), F32)
        for i in range(3):
            for j in range(4):
                lhs = jnp.where(row == i * 4 + j, split[j][i].astype(F32), lhs)
        v = dot_nn(lhs.astype(BF16), tok_in[...])
        rgs[...] = v[0:4, :] + v[4:8, :] + v[8:12, :]
        for k in range(1, 8):
            cp.add(("rg", k), rgs, rgr.at[k], {"dp": (z + k) % 8})
        i0 = lax.broadcasted_iota(jnp.int32, (128, 128), 0)
        i1 = lax.broadcasted_iota(jnp.int32, (128, 128), 1)
        eye_t = (i0 == i1).astype(F32)

        def col_t(row):
            return jnp.sum(eye_t * row, axis=1, keepdims=True)

        lane = lax.broadcasted_iota(jnp.int32, (128, 16), 1)
        of_expert = (lane % 4).astype(F32)
        v = (jnp.where(col_t(e0.astype(F32)) == of_expert, col_t(w0), 0.0)
             + jnp.where(col_t(e1.astype(F32)) == of_expert, col_t(w1), 0.0))
        hi, mid, low = (q.astype(F32) for q in parts3(v))
        lg3[...] = jnp.where(lane < 4, hi, jnp.where(lane < 8, mid, jnp.where(lane < 12, low, 0.0)))

    def router_5():
        total = rgs[...]
        for k in range(1, 8):
            cp.got(("rg", k))
            total = total + rgr[k]
        router_out[...] = total

    def finish():
        rows = pl.ds(pl.multiple_of(y * 32, 32), 32)
        total = own_q[...]
        total = total + dot_nn(lg3[rows, :].astype(BF16), jnp.concatenate([rwt[...]] * 4, axis=0))
        for p in range(8):
            o = BLOCKS[p]
            if o != 0:
                cp.got(("z", -o if o != 4 else 4))
                total = total + zq[p].astype(F32)
        tok_out[...] = total.astype(BF16)

    def weights(m, i):
        out, left_side, right_side = (
            (gg_o, tk, hh.at[1]), (ug_o, tk, hh.at[2]), (dg_o, hh.at[0], sc))[m]
        size = out.shape[0] // 3 if m < 2 else out.shape[0] // 4
        rows = slice(i * size, i * size + size)
        out[rows, :] = lax.dot_general(
            left_side[:, rows], right_side[...], (((0,), (0,)), ((), ())),
            preferred_element_type=F32).astype(BF16)

    run = {
        "open": open_up, "prob": probabilities, "far": far, "Z": pass_on, "F": forward, "D": to_sibling,
        "R1": reduce_1, "R2": reduce_2, "E": activate, "G": spread, "X": backward,
        "Y": homeward, "P1": router_1, "P3": router_3,
        "P5": router_5, "S": tables, "V": relay, "W": weights, "end": finish,
    }
    for step in STEPS:
        run[step[0]](*step[1:])
    cp.drain()


def put_out(*refs):
    sem = refs[10]
    copies = [pltpu.make_async_copy(refs[i], refs[5 + i], sem.at[i]) for i in range(5)]
    for q in copies:
        q.start()
    for q in copies:
        q.wait()


def shards(
    tokens, out_grad, router_weight, gate_weight, up_weight, down_weight, expert_index, slot_index
):
    vm = pl.BlockSpec(memory_space=pltpu.VMEM)
    hbm = pl.BlockSpec(memory_space=pltpu.HBM)
    V = pltpu.VMEM
    small = V((8, 128), F32)
    several = V((8, 8, 128), F32)
    out_shape = [
        jax.ShapeDtypeStruct((32, 768), BF16),
        jax.ShapeDtypeStruct((4, 768), F32),
        jax.ShapeDtypeStruct((768, 1024), BF16),
        jax.ShapeDtypeStruct((768, 1024), BF16),
        jax.ShapeDtypeStruct((1024, 768), BF16),
    ]
    results = pl.pallas_call(
        kernel,
        name="moe_backward",
        in_specs=[hbm] * 8,
        out_specs=[vm] * 5,
        out_shape=out_shape,
        scratch_shapes=[
            V((768, 768), BF16), V((768, 768), BF16), V((768, 768), BF16),
            V((768, 1024), BF16), V((768, 1024), BF16), V((1024, 768), BF16),
            V((2, 4, 768, 384), BF16), V((4, 768, 384), BF16),
            V((768, 384), BF16), V((768, 384), BF16), V((768, 384), BF16), V((768, 384), BF16),
            V((3, 768, 1024), BF16), V((768, 1), F32), V((768, 1), F32),
            small, several, small, several, several, several, V((8, 8, 128), jnp.int32),
            V((8, 128, CAP), BF16), V((768, 768), BF16), V((8, 32, 768), BF16),
            V((8, 32, 768), BF16), V((32, 768), F32),
            small, V((32, 8, 128), F32), V((4, 768), F32), V((8, 4, 768), F32), V((128, 16), F32),
            V((128, 768), BF16), V((128, 768), BF16), V((4, 768), BF16),
            V((2, 128), jnp.int32), V((2, 128), jnp.int32),
            pltpu.SemaphoreType.DMA((N_COPIES,)), pltpu.SemaphoreType.DMA((N_COPIES,)),
            pltpu.SemaphoreType.DMA((8,)),
            *(V((sum(GROUPS[k0 : k0 + n]) // 2, rows, 768), BF16)
              for rows in (128, 16, 16, 32, 32) for k0, n in BACKS),
        ],
        compiler_params=pltpu.CompilerParams(
            collective_id=0, has_side_effects=True, vmem_limit_bytes=40 * 1024 * 1024
        ),
    )(
        *(pltpu.with_memory_space_constraint(v, pltpu.HBM) for v in (
            tokens, out_grad, router_weight.T, expert_index.T, slot_index.T,
            gate_weight[0], up_weight[0], down_weight[0],
        ))
    )
    tokens_grad, router_grad, gate_grad, up_grad, down_grad = pl.pallas_call(
        put_out,
        name="put_out",
        in_specs=[vm] * 5,
        out_specs=[hbm] * 5,
        out_shape=out_shape,
        scratch_shapes=[pltpu.SemaphoreType.DMA((5,))],
        compiler_params=pltpu.CompilerParams(vmem_limit_bytes=1024 * 1024),
    )(*results)
    return (tokens_grad, router_grad.T, gate_grad[None], up_grad[None], down_grad[None])


def solution(mesh):
    in_specs = (
        P("dp", "tensor"),
        P("dp", "tensor"),
        P("tensor", None),
        P("expert", "tensor", "dp"),
        P("expert", "tensor", "dp"),
        P("expert", "dp", "tensor"),
        P("dp", None),
        P("dp", None),
    )
    out_specs = (
        P(("dp", "expert"), "tensor"),
        P("tensor", None),
        P("expert", "tensor", "dp"),
        P("expert", "tensor", "dp"),
        P("expert", "dp", "tensor"),
    )
    return jax.shard_map(shards, mesh=mesh, in_specs=in_specs, out_specs=out_specs, check_vma=False)
```

time: 92.8 us -> 84.7 us (0.913)
  Pallas kernels: 92 us -> 83.4 us
    pallas_call x1, Pallas kernels: 89.7 us -> 81.1 us  [shards(): pl.pallas_call(kernel, name='moe_backward', in_specs=[hbm] * 8, out_specs...]
where the time goes in v4:
time: 84.7 us; the launch traced here: 84.2 us
  Pallas kernels  83.4 us (98%)
    pallas_call x1, Pallas kernels, shards(): pl.pallas_call(kernel, name='moe_backward', in_specs=[hbm] * 8, out_specs...  81.1 us
    pallas_call x1, Pallas kernels, shards(): pl.pallas_call(put_out, name='put_out', in_specs=[vm] * 5, out_specs=[hbm...  2.25 us

profile of v4, /device:TPU:1, one launch (start us, length us, event | category | flops | bytes accessed | tf_op | source)
XLA Modules:
  0.0 84.2 jit_solution(16341878555293701678)
XLA Ops:
  0.6 81.1 %moe_backward.1 = (bf16[32,768]{1,0:T(8,128)(2,1)S(1)}, f32[4,768]{1,0:T(4,128)S(1)}, bf16[768,1024]{1,0:T(8,128)(2,1)S(1)}, bf16[768,1024]{1,0:T(8,128)(2,1)S(1)}, bf16[1024,768]{1,0:T(8,128)(2,1)S(1)}) custom-call(bf16[128,768]{1,0:T(8,128)(2,1)} %tok_h.1, bf16[128,768]{1,0:T(8,128)(2,1)} %og_h.1, bf16[4,768]{1,0:T(4,128)(2,1)} %bitcast.13, ...), custom_call_target="tpu_custom_call" | custom-call | tf_op jit(solution)/shard_map/moe_backward/pallas_call | solution.py:566
  81.8 2.2 %put_out.1 = (bf16[32,768]{1,0:T(8,128)(2,1)}, f32[4,768]{1,0:T(4,128)}, bf16[768,1024]{1,0:T(8,128)(2,1)}, bf16[768,1024]{1,0:T(8,128)(2,1)}, bf16[1024,768]{1,0:T(8,128)(2,1)}) custom-call(bf16[32,768]{1,0:T(8,128)(2,1)S(1)} %get-tuple-element.15.refs_0_, f32[4,768]{1,0:T(4,128)S(1)} %get-tuple-element.16.refs_1_, ...), custom_call_target="tpu_custom_call" | custom-call | tf_op jit(solution)/shard_map/put_out/pallas_call | solution.py:598

commit v5 on v4

--- a/solution.py
+++ b/solution.py
@@ -79,31 +79,41 @@
 
 class Copies:
     def __init__(self, send, recv):
-        self.send, self.recv, self.count, self.made = send, recv, 0, {}
-
-    def add(self, name, src, dst, device):
-        i = self.count
-        self.count += 1
-        c = pltpu.make_async_remote_copy(
+        self.send, self.recv, self.at, self.made, self.sent = send, recv, {}, {}, []
+
+    def describe(self, key, src, dst, device, slot):
+        i = self.at.setdefault(key, len(self.at))
+        return pltpu.make_async_remote_copy(
             src_ref=src,
             dst_ref=dst,
-            send_sem=self.send.at[i],
+            send_sem=self.send.at[slot],
             recv_sem=self.recv.at[i],
             device_id=device,
             device_id_type=MESH,
         )
+
+    def add(self, name, src, dst, device, group=None):
+        slot = len(self.sent) % N_SEND
+        if len(self.sent) >= N_SEND:
+            self.sent[-N_SEND].wait_send()
+        c = self.describe(group or name, src, dst, device, slot)
+        self.sent.append(c)
         self.made[name] = c
         c.start()
 
     def got(self, name):
         self.made[name].wait_recv()
 
+    def got_all(self, group, ref, device):
+        self.describe(group, ref, ref, device, 0).wait_recv()
+
     def drain(self):
-        for c in self.made.values():
+        for c in self.sent[-N_SEND:]:
             c.wait_send()
 
 
-N_COPIES = 340
+N_SEND = 32
+N_RECV = 155
 
 
 def kernel(
@@ -169,12 +179,17 @@
     def ring(step, half):
         for which, buf in (("t", tk), ("g", gr)):
             cp.add(("r", step + 1, half, which), buf.at[pl.ds(ROW[near(-step), half], HALF)],
-                   buf.at[pl.ds(ROW[near(-step - 1), half], HALF)], {"dp": (z + 1) % 8})
+                   buf.at[pl.ds(ROW[near(-step - 1), half], HALF)], {"dp": (z + 1) % 8},
+                   ("r", step + 1, half))
 
     def ring_back(step, half):
         for which, buf in (("t", tk), ("g", gr)):
             cp.add(("l", step + 1, half, which), buf.at[pl.ds(ROW[near(step), half], HALF)],
-                   buf.at[pl.ds(ROW[near(step + 1), half], HALF)], {"dp": (z + 7) % 8})
+                   buf.at[pl.ds(ROW[near(step + 1), half], HALF)], {"dp": (z + 7) % 8},
+                   ("l", step + 1, half))
+
+    def piece_in(way, step, half):
+        cp.got_all((way, step, half), tk.at[pl.ds(0, CAP)], {"dp": (z + 1) % 8})
 
     def to_col(row):
         return jnp.sum(eye * row, axis=1, keepdims=True)
@@ -206,12 +221,12 @@
             ring(0, half)
             ring_back(0, half)
         for k in range(1, 8):
-            cp.add(("lg", k), lgs, lgr.at[k], {"tensor": (t + k) % 8})
+            cp.add(("lg", k), lgs, lgr.at[k], {"tensor": (t + k) % 8}, "lg")
 
     def probabilities():
         total = lgs[0:4, :]
+        cp.got_all("lg", lgr.at[pl.ds(1, 7)], {"tensor": t_sib})
         for k in range(1, 8):
-            cp.got(("lg", k))
             total = total + lgr[k][0:4, :]
         l0 = jnp.zeros((1, 128), F32)
         l1 = jnp.zeros((1, 128), F32)
@@ -235,12 +250,10 @@
             cp.add(("pr", k), prs, prr.at[place(-k)], {"dp": (z + k) % 8})
 
     def pass_on(d, half):
-        for which in "tg":
-            cp.got(("r", d, half, which))
+        piece_in("r", d, half)
         if d < 3 or half == 0:
             ring(d, half)
-        for which in "tg":
-            cp.got(("l", d, half, which))
+        piece_in("l", d, half)
         if d < 3 or half == 1:
             ring_back(d, half)
 
@@ -269,8 +282,7 @@
             ready.append(1)
         for o, half in units_in(k):
             if j == 2 and o == 4:
-                for which in "tg":
-                    cp.got(("rl"[half], 4, half, which))
+                piece_in("rl"[half], 4, half)
         a = tk[r0 : r0 + r, :]
         b = gr[r0 : r0 + r, :]
         q = turn[j]
@@ -304,28 +316,28 @@
             cp.add(("fb", k), part.at[c, across, db, :], fb.at[db, :], {"tensor": t_left})
         if j == 1:
             fold(right, sb)
-            cp.add(("rlb", k), part.at[c, right, db, :], rl.at[db, :], {"tensor": t_right})
+            cp.add(("rlb", k), part.at[c, right, db, :], rl.at[db, :], {"tensor": t_right}, ("rs", k))
         if j == 3:
             fold(left, sa)
-            cp.add(("rra", k), part.at[c, left, da, :], rr.at[da, :], {"tensor": t_left})
+            cp.add(("rra", k), part.at[c, left, da, :], rr.at[da, :], {"tensor": t_left}, ("rs", k))
 
     def reduce_2(k, side):
         sa, sb, da, db = halves(k)
         if side == 0:
             cp.got(("fa", k))
             fold(right, sa, fa)
-            cp.add(("rla", k), part.at[c, right, da, :], rl.at[da, :], {"tensor": t_right})
+            cp.add(("rla", k), part.at[c, right, da, :], rl.at[da, :], {"tensor": t_right}, ("rs", k))
         else:
             cp.got(("fb", k))
             fold(left, sb, fb)
-            cp.add(("rrb", k), part.at[c, left, db, :], rr.at[db, :], {"tensor": t_left})
+            cp.add(("rrb", k), part.at[c, left, db, :], rr.at[db, :], {"tensor": t_left}, ("rs", k))
 
     def tcols(q):
         return pl.ds(pl.multiple_of(q * 128, 128), 128)
 
-    def h_copy(name, rows, q, device):
+    def h_copy(name, rows, q, device, group=None):
         ref = hh.at[:, rows, tcols(q)]
-        cp.add(name, ref, ref, {"tensor": device})
+        cp.add(name, ref, ref, {"tensor": device}, group)
 
     def activate(k):
         sa, sb, da, db = halves(k)
@@ -338,9 +350,8 @@
                     pcol[ROW[o, i] : ROW[o, i] + HALF, :] = col[i * HALF : (i + 1) * HALF, :]
         cp.got(("d", k, 0))
         sums = []
-        for s, names in ((sb, ("rlb", "rrb")), (sa, ("rla", "rra"))):
-            for q in names:
-                cp.got((q, k))
+        cp.got_all(("rs", k), dbuf.at[pl.ds(0, 2), pl.ds(*rows_in(k)), :], {"tensor": t_sib})
+        for s in (sb, sa):
             v = part[c, x, s, :].astype(F32) + dbuf[x, s, :].astype(F32)
             v = v + rl[s, :].astype(F32) + rr[s, :].astype(F32)
             gate, up, ga = v[:, 0:128], v[:, 128:256], v[:, 256:384]
@@ -355,7 +366,7 @@
         h_copy(("lb", k), db, t, t_left)
         h_copy(("rb", k), db, t, t_right)
         h_copy(("la", k), da, t, t_left)
-        h_copy(("so", k), pl.ds(*rows_in(k)), t, t_sib)
+        h_copy(("so", k), pl.ds(*rows_in(k)), t, t_sib, ("s", k))
         dcol[sa, :] = sums[0]
         dcol[sb, :] = sums[1]
         for o, half in units_in(k):
@@ -366,7 +377,7 @@
                 p = POS[o]
                 dps[p] = jnp.broadcast_to(to_row(col), (8, 128))
                 if o != 0:
-                    cp.add(("dp", o), dps.at[p], dpr.at[place(-o)], {"dp": (z + o) % 8})
+                    cp.add(("dp", o), dps.at[p], dpr.at[place(-o)], {"dp": (z + o) % 8}, "dp")
         r0, r = rows_in(k)
         s = slice(r0, r0 + r)
         sc[s, :] = (pcol[s, :] * gr[s, :].astype(F32)).astype(BF16)
@@ -376,20 +387,19 @@
         full = pl.ds(*rows_in(k))
         if i == 0:
             cp.got(("ra", k))
-            h_copy(("xa", k), da, t_left, t_right)
+            h_copy(("xa", k), da, t_left, t_right, ("x", k))
         if i == 1:
             cp.got(("lb", k))
-            h_copy(("xb", k), db, t_right, t_left)
+            h_copy(("xb", k), db, t_right, t_left, ("x", k))
         if i == 2:
             cp.got(("rb", k))
-            h_copy(("sl", k), full, t_left, t_sib)
+            h_copy(("sl", k), full, t_left, t_sib, ("s", k))
         if i == 3:
             cp.got(("la", k))
-            h_copy(("sr", k), full, t_right, t_sib)
+            h_copy(("sr", k), full, t_right, t_sib, ("s", k))
         if i == 4:
-            cp.got(("xa", k))
-            cp.got(("xb", k))
-            h_copy(("sx", k), full, across * 2 + c, t_sib)
+            cp.got_all(("x", k), hh.at[:, full, pl.ds(0, 128)], {"tensor": t_sib})
+            h_copy(("sx", k), full, across * 2 + c, t_sib, ("s", k))
 
     def tables(p):
         o = BLOCKS[p]
@@ -408,8 +418,7 @@
 
     def backward(m):
         for k in chunks_in(m):
-            for q in ("so", "sl", "sr", "sx"):
-                cp.got((q, k))
+            cp.got_all(("s", k), hh.at[:, pl.ds(*rows_in(k)), pl.ds(0, 512)], {"tensor": t_sib})
         r0 = rows_in(chunks_in(m)[0])[0]
         r = sum(rows_in(k)[1] for k in chunks_in(m))
         a = hh[1, r0 : r0 + r, :]
@@ -426,8 +435,10 @@
 
         cp.add(("ya", m), piece(2, 0), ya[m], {"expert": (y + 1) % 4})
         cp.add(("yb", m), piece(2, 16), yb[m], {"expert": (y + 3) % 4})
-        cp.add(("yr", m), piece(1, 16), yr[m].at[:, pl.ds(16, 16), :], {"expert": (y + 1) % 4})
-        cp.add(("yl", m), piece(3, 0), yl[m].at[:, pl.ds(0, 16), :], {"expert": (y + 3) % 4})
+        cp.add(("yr", m), piece(1, 16), yr[m].at[:, pl.ds(16, 16), :], {"expert": (y + 1) % 4},
+               ("yy", m))
+        cp.add(("yl", m), piece(3, 0), yl[m].at[:, pl.ds(0, 16), :], {"expert": (y + 3) % 4},
+               ("yy", m))
 
     def relay(m):
         for name, q, low, buf, put in (("ya", 1, 0, ya, yr), ("yb", 3, 16, yb, yl)):
@@ -437,11 +448,11 @@
                 yd[m][i, rows, :] = (
                     yd[m][i, rows, :].astype(F32) + buf[m][i].astype(F32)).astype(BF16)
             cp.add((name, m, 2), yd[m].at[:, rows, :], put[m].at[:, pl.ds(low, 16), :],
-                   {"expert": (y + q) % 4})
+                   {"expert": (y + q) % 4}, ("yy", m))
 
     def homeward(m):
-        for name in (("yr", m), ("yl", m), ("ya", m, 2), ("yb", m, 2)):
-            cp.got(name)
+        n = len(blocks_in(m))
+        cp.got_all(("yy", m), yd[m].at[pl.ds(0, n), pl.ds(0, 64), :], {"expert": (y + 1) % 4})
         rows = pl.ds(pl.multiple_of(y * 32, 32), 32)
         for i, o in enumerate(blocks_in(m)):
             v = yd[m][i, rows, :].astype(F32) + yr[m][i].astype(F32) + yl[m][i].astype(F32)
@@ -449,26 +460,23 @@
                 own_q[...] = v
             else:
                 yq[POS[o]] = v.astype(BF16)
-                cp.add(("z", o), yq.at[POS[o]], zq.at[place(-o)], {"dp": (z + o) % 8})
+                cp.add(("z", o), yq.at[POS[o]], zq.at[place(-o)], {"dp": (z + o) % 8}, "z")
 
     def router_1():
         total = dps[0][0:1, :]
-        for p in range(8):
-            if BLOCKS[p] != 0:
-                o = BLOCKS[p]
-                cp.got(("dp", -o if o != 4 else 4))
-                total = total + dpr[p][0:1, :]
+        cp.got_all("dp", dpr.at[pl.ds(1, 7)], {"dp": (z + 1) % 8})
+        for p in range(1, 8):
+            total = total + dpr[p][0:1, :]
         col = to_col(total)
         pts[...] = rows8(jnp.sum(table0 * col, axis=0, keepdims=True),
                          jnp.sum(table1 * col, axis=0, keepdims=True))
         for k in range(1, 32):
             cp.add(("pt", k), pts, ptr.at[k],
-                   {"expert": (y + k // 8) % 4, "tensor": (t + k) % 8})
+                   {"expert": (y + k // 8) % 4, "tensor": (t + k) % 8}, "pt")
 
     def router_3():
         total = pts[...]
-        for k in range(1, 32):
-            cp.got(("pt", k))
+        cp.got_all("pt", ptr.at[pl.ds(1, 31)], {"tensor": t_sib})
         for k in range(1, 32):
             total = total + ptr[k]
         d0, d1 = total[0:1, :], total[1:2, :]
@@ -486,7 +494,7 @@
         v = dot_nn(lhs.astype(BF16), tok_in[...])
         rgs[...] = v[0:4, :] + v[4:8, :] + v[8:12, :]
         for k in range(1, 8):
-            cp.add(("rg", k), rgs, rgr.at[k], {"dp": (z + k) % 8})
+            cp.add(("rg", k), rgs, rgr.at[k], {"dp": (z + k) % 8}, "rg")
         i0 = lax.broadcasted_iota(jnp.int32, (128, 128), 0)
         i1 = lax.broadcasted_iota(jnp.int32, (128, 128), 1)
         eye_t = (i0 == i1).astype(F32)
@@ -503,20 +511,19 @@
 
     def router_5():
         total = rgs[...]
+        cp.got_all("rg", rgr.at[pl.ds(1, 7)], {"dp": (z + 1) % 8})
         for k in range(1, 8):
-            cp.got(("rg", k))
             total = total + rgr[k]
         router_out[...] = total
 
     def finish():
+        cp.drain()
         rows = pl.ds(pl.multiple_of(y * 32, 32), 32)
         total = own_q[...]
         total = total + dot_nn(lg3[rows, :].astype(BF16), jnp.concatenate([rwt[...]] * 4, axis=0))
-        for p in range(8):
-            o = BLOCKS[p]
-            if o != 0:
-                cp.got(("z", -o if o != 4 else 4))
-                total = total + zq[p].astype(F32)
+        cp.got_all("z", zq.at[pl.ds(1, 7)], {"dp": (z + 1) % 8})
+        for p in range(1, 8):
+            total = total + zq[p].astype(F32)
         tok_out[...] = total.astype(BF16)
 
     def weights(m, i):
@@ -536,7 +543,6 @@
     }
     for step in STEPS:
         run[step[0]](*step[1:])
-    cp.drain()
 
 
 def put_out(*refs):
@@ -581,7 +587,7 @@
             small, V((32, 8, 128), F32), V((4, 768), F32), V((8, 4, 768), F32), V((128, 16), F32),
             V((128, 768), BF16), V((128, 768), BF16), V((4, 768), BF16),
             V((2, 128), jnp.int32), V((2, 128), jnp.int32),
-            pltpu.SemaphoreType.DMA((N_COPIES,)), pltpu.SemaphoreType.DMA((N_COPIES,)),
+            pltpu.SemaphoreType.DMA((N_SEND,)), pltpu.SemaphoreType.DMA((N_RECV,)),
             pltpu.SemaphoreType.DMA((8,)),
             *(V((sum(GROUPS[k0 : k0 + n]) // 2, rows, 768), BF16)
               for rows in (128, 16, 16, 32, 32) for k0, n in BACKS),

time: 84.7 us -> 81 us (0.956)
  Pallas kernels: 83.4 us -> 79.3 us
    pallas_call x1, Pallas kernels: 81.1 us -> 77.1 us  [shards(): pl.pallas_call(kernel, name='moe_backward', in_specs=[hbm] * 8, out_specs...]
where the time goes in v5:
time: 81 us; the launch traced here: 80.1 us
  Pallas kernels  79.3 us (98%)
    pallas_call x1, Pallas kernels, shards(): pl.pallas_call(kernel, name='moe_backward', in_specs=[hbm] * 8, out_specs...  77.1 us
    pallas_call x1, Pallas kernels, shards(): pl.pallas_call(put_out, name='put_out', in_specs=[vm] * 5, out_specs=[hbm...  2.25 us

profile of v5, /device:TPU:1, one launch (start us, length us, event | category | flops | bytes accessed | tf_op | source)
XLA Modules:
  0.0 80.1 jit_solution(8379284600759617256)
XLA Ops:
  0.6 77.1 %moe_backward.1 = (bf16[32,768]{1,0:T(8,128)(2,1)S(1)}, f32[4,768]{1,0:T(4,128)S(1)}, bf16[768,1024]{1,0:T(8,128)(2,1)S(1)}, bf16[768,1024]{1,0:T(8,128)(2,1)S(1)}, bf16[1024,768]{1,0:T(8,128)(2,1)S(1)}) custom-call(bf16[128,768]{1,0:T(8,128)(2,1)} %tok_h.1, bf16[128,768]{1,0:T(8,128)(2,1)} %og_h.1, bf16[4,768]{1,0:T(4,128)(2,1)} %bitcast.13, ...), custom_call_target="tpu_custom_call" | custom-call | tf_op jit(solution)/shard_map/moe_backward/pallas_call | solution.py:572
  77.7 2.2 %put_out.1 = (bf16[32,768]{1,0:T(8,128)(2,1)}, f32[4,768]{1,0:T(4,128)}, bf16[768,1024]{1,0:T(8,128)(2,1)}, bf16[768,1024]{1,0:T(8,128)(2,1)}, bf16[1024,768]{1,0:T(8,128)(2,1)}) custom-call(bf16[32,768]{1,0:T(8,128)(2,1)S(1)} %get-tuple-element.15.refs_0_, f32[4,768]{1,0:T(4,128)S(1)} %get-tuple-element.16.refs_1_, ...), custom_call_target="tpu_custom_call" | custom-call | tf_op jit(solution)/shard_map/put_out/pallas_call | solution.py:604

commit v6 on v5

--- a/solution.py
+++ b/solution.py
@@ -62,10 +62,10 @@
     ("R2", 7, 0), ("R2", 7, 1), ("X", 2), ("E", 6), ("V", 1), ("S", 6), ("S", 7), ("G", 5, 0),
     ("G", 5, 1), ("G", 5, 2), ("G", 5, 3), ("E", 7), ("G", 6, 0), ("G", 6, 1), ("V", 2),
     ("G", 6, 2), ("G", 6, 3), ("G", 5, 4), ("Y", 1), ("G", 7, 0), ("G", 7, 1), ("X", 3),
-    ("G", 7, 2), ("G", 6, 4), ("G", 7, 3), ("Y", 2), ("P1",), ("G", 7, 4), ("X", 4), ("V", 3),
-    ("X", 5), ("W", 0, 0), ("P3",), ("W", 0, 1), ("V", 4), ("W", 0, 2), ("W", 1, 0), ("Y", 3),
-    ("W", 1, 1), ("V", 5), ("W", 1, 2), ("W", 2, 0), ("W", 2, 1), ("Y", 4), ("W", 2, 2),
-    ("W", 2, 3), ("Y", 5), ("P5",), ("end",),
+    ("G", 7, 2), ("G", 6, 4), ("G", 7, 3), ("Y", 2), ("G", 7, 4), ("P1",), ("X", 4), ("X", 5),
+    ("W", 0, 0), ("Y", 3), ("W", 0, 1), ("W", 0, 2), ("V", 4), ("P3",), ("W", 1, 0), ("W", 1, 1),
+    ("W", 1, 2), ("Y", 5), ("Y", 4), ("W", 2, 0), ("W", 2, 1), ("W", 2, 2), ("W", 2, 3), ("P5",),
+    ("end",),
 )
 
 
@@ -94,10 +94,13 @@
 
     def add(self, name, src, dst, device, group=None):
         slot = len(self.sent) % N_SEND
-        if len(self.sent) >= N_SEND:
+        if group == "pt":
+            slot = N_SEND
+        elif len(self.sent) >= N_SEND:
             self.sent[-N_SEND].wait_send()
         c = self.describe(group or name, src, dst, device, slot)
-        self.sent.append(c)
+        if slot < N_SEND:
+            self.sent.append(c)
         self.made[name] = c
         c.start()
 
@@ -112,7 +115,8 @@
             c.wait_send()
 
 
-N_SEND = 32
+DIRECT = (3, 5)
+N_SEND = 40
 N_RECV = 155
 
 
@@ -124,7 +128,7 @@
     pts, ptr, rgs, rgr, lg3,
     tok_in, og_in, rwt, ex, sl, send_sem, recv_sem, wsem, *sums,
 ):
-    yd, ya, yb, yr, yl = (sums[i * len(BACKS) : (i + 1) * len(BACKS)] for i in range(5))
+    yd, ya, yb, yr, yl, yx = (sums[i * len(BACKS) : (i + 1) * len(BACKS)] for i in range(6))
     z = lax.axis_index("dp")
     y = lax.axis_index("expert")
     t = lax.axis_index("tensor")
@@ -430,6 +434,12 @@
             v = jnp.concatenate([dxs[ROW[o, h] : ROW[o, h] + HALF, :] for h in range(2)], axis=0)
             yd[m][i] = dot_nn(selt[POS[o]], v).astype(BF16)
 
+        if m in DIRECT:
+            for q, put in ((2, yx[m]), (1, yr[m]), (3, yl[m])):
+                rows = pl.ds(pl.multiple_of(((y + q) % 4) * 32, 32), 32)
+                cp.add(("y", m, q), yd[m].at[:, rows, :], put, {"expert": (y + q) % 4}, ("yy", m))
+            return
+
         def piece(q, low):
             return yd[m].at[:, pl.ds(pl.multiple_of(((y + q) % 4) * 32 + low, 16), 16), :]
 
@@ -452,10 +462,13 @@
 
     def homeward(m):
         n = len(blocks_in(m))
-        cp.got_all(("yy", m), yd[m].at[pl.ds(0, n), pl.ds(0, 64), :], {"expert": (y + 1) % 4})
+        cp.got_all(("yy", m), yd[m].at[pl.ds(0, n), pl.ds(0, 96 if m in DIRECT else 64), :],
+                   {"expert": (y + 1) % 4})
         rows = pl.ds(pl.multiple_of(y * 32, 32), 32)
         for i, o in enumerate(blocks_in(m)):
             v = yd[m][i, rows, :].astype(F32) + yr[m][i].astype(F32) + yl[m][i].astype(F32)
+            if m in DIRECT:
+                v = v + yx[m][i].astype(F32)
             if o == 0:
                 own_q[...] = v
             else:
@@ -518,6 +531,8 @@
 
     def finish():
         cp.drain()
+        many = ptr.at[pl.ds(1, 31)]
+        cp.describe("pt", many, many, {"tensor": t_sib}, N_SEND).wait_send()
         rows = pl.ds(pl.multiple_of(y * 32, 32), 32)
         total = own_q[...]
         total = total + dot_nn(lg3[rows, :].astype(BF16), jnp.concatenate([rwt[...]] * 4, axis=0))
@@ -587,10 +602,10 @@
             small, V((32, 8, 128), F32), V((4, 768), F32), V((8, 4, 768), F32), V((128, 16), F32),
             V((128, 768), BF16), V((128, 768), BF16), V((4, 768), BF16),
             V((2, 128), jnp.int32), V((2, 128), jnp.int32),
-            pltpu.SemaphoreType.DMA((N_SEND,)), pltpu.SemaphoreType.DMA((N_RECV,)),
+            pltpu.SemaphoreType.DMA((N_SEND + 1,)), pltpu.SemaphoreType.DMA((N_RECV,)),
             pltpu.SemaphoreType.DMA((8,)),
             *(V((sum(GROUPS[k0 : k0 + n]) // 2, rows, 768), BF16)
-              for rows in (128, 16, 16, 32, 32) for k0, n in BACKS),
+              for rows in (128, 16, 16, 32, 32, 32) for k0, n in BACKS),
         ],
         compiler_params=pltpu.CompilerParams(
             collective_id=0, has_side_effects=True, vmem_limit_bytes=40 * 1024 * 1024

time: 81 us -> 79.6 us (0.983); the launches traced: 80.1 us -> 79.5 us
  no operation moved by 1% of the time
where the time goes in v6:
time: 79.6 us; the launch traced here: 79.5 us
  Pallas kernels  78.7 us (99%)
  between operations  0.8 us (1%)
    pallas_call x1, Pallas kernels, shards(): pl.pallas_call(kernel, name='moe_backward', in_specs=[hbm] * 8, out_specs...  76.5 us
    pallas_call x1, Pallas kernels, shards(): pl.pallas_call(put_out, name='put_out', in_specs=[vm] * 5, out_specs=[hbm...  2.25 us

profile of v6, /device:TPU:1, one launch (start us, length us, event | category | flops | bytes accessed | tf_op | source)
XLA Modules:
  0.0 79.5 jit_solution(8744342944590886911)
XLA Ops:
  0.6 76.5 %moe_backward.1 = (bf16[32,768]{1,0:T(8,128)(2,1)S(1)}, f32[4,768]{1,0:T(4,128)S(1)}, bf16[768,1024]{1,0:T(8,128)(2,1)S(1)}, bf16[768,1024]{1,0:T(8,128)(2,1)S(1)}, bf16[1024,768]{1,0:T(8,128)(2,1)S(1)}) custom-call(bf16[128,768]{1,0:T(8,128)(2,1)} %tok_h.1, bf16[128,768]{1,0:T(8,128)(2,1)} %og_h.1, bf16[4,768]{1,0:T(4,128)(2,1)} %bitcast.13, ...), custom_call_target="tpu_custom_call" | custom-call | tf_op jit(solution)/shard_map/moe_backward/pallas_call | solution.py:587
  77.1 2.2 %put_out.1 = (bf16[32,768]{1,0:T(8,128)(2,1)}, f32[4,768]{1,0:T(4,128)}, bf16[768,1024]{1,0:T(8,128)(2,1)}, bf16[768,1024]{1,0:T(8,128)(2,1)}, bf16[1024,768]{1,0:T(8,128)(2,1)}) custom-call(bf16[32,768]{1,0:T(8,128)(2,1)S(1)} %get-tuple-element.15.refs_0_, f32[4,768]{1,0:T(4,128)S(1)} %get-tuple-element.16.refs_1_, ...), custom_call_target="tpu_custom_call" | custom-call | tf_op jit(solution)/shard_map/put_out/pallas_call | solution.py:619
